TPU v7x, 128 devices: a whole 4x4x4 slice. The times are simulated.
128 devices in a mesh: gx: 16 (over y, x_hi, core), gy: 8 (over z, x_lo).
Axes of the slice: x: 4 (x_hi: 2, x_lo: 2; x = x_hi * 2 + x_lo), y: 4, z: 4, core: 2. Of those that a mesh axis runs over, the one named last changes fastest.
Arguments:
- velocity: float32 [2, 640, 2048], P(None, 'gy', 'gx'), may hold values from -4 to 4
- stress: float32 [3, 640, 2048], P(None, 'gy', 'gx'), may hold values from -6 to 6
- wind: float32 [2, 640, 2048], P(None, 'gy', 'gx'), may hold values from -4 to 4
- strength: float32 [640, 2048], P('gy', 'gx'), may hold values from 0.5 to 2
- mass: float32 [640, 2048], P('gy', 'gx'), may hold values from 0.5 to 2
- land_mask: int32 [640, 2048], P('gy', 'gx'), may hold values 0 or 1
- region_mask: int32 [640, 2048], P('gy', 'gx'), may hold values 0 or 1
- observed: float32 [2, 640, 2048], P(None, 'gy', 'gx'), may hold values from -4 to 4
- start_index: int32 [1], replicated, may hold values from 0 to 112
Outputs:
- state_adjoint: float32 [5, 640, 2048], P(None, 'gy', 'gx')
- wind_direction: float32 [2, 640, 2048], P(None, 'gy', 'gx')
All inputs are finite; a program needn't handle non-finite values. No bound on the sum of `land_mask` or of `region_mask` on one device may be relied on, other than what follows from the above.
Results may differ from a plain program's by a relative error of at most 0.00002.
Values sent between devices are 32-bit elements; how exact they have to be, the bound alone decides.
A program may use at most 64 MiB of HBM per device.

v0:
```python
import jax
import jax.numpy as jnp
from jax import lax
from jax.sharding import Mesh
from jax.sharding import PartitionSpec as P

STEPS = 8
SUBTOTAL = 120
GY = ("gy_0", "gy_1")
GX = ("gx_0", "gx_1", "gx_2")
GX_GY = ("gx_0", "gx_1", "gx_2", "gy_0", "gy_1")


ellipse_sq = 4.0
delta_floor = 0.04
time_step = 0.5
drag_rate = 1.0
norm_eps = 1e-06


def with_halo(block, sides, width, periodic):
    for axis, dim in sides:
        count = lax.axis_size(axis)
        forward = [(i, i + 1) for i in range(count - 1)]
        if periodic:
            forward.append((count - 1, 0))
        backward = [(target, source) for source, target in forward]
        low = lax.ppermute(
            lax.slice_in_dim(block, block.shape[dim] - width, None, axis=dim), axis, forward
        )
        high = lax.ppermute(lax.slice_in_dim(block, 0, width, axis=dim), axis, backward)
        block = jnp.concatenate([low, block, high], axis=dim)
    return block


def from_everyone(value, axis):
    copies = jnp.broadcast_to(value, (lax.axis_size(axis), *value.shape))
    return lax.all_to_all(copies, axis, split_axis=0, concat_axis=0, tiled=True)


def in_order(blocks, dim):
    blocks = jnp.moveaxis(blocks, 0, dim)
    lengths = blocks.shape
    return blocks.reshape(*lengths[:dim], lengths[dim] * lengths[dim + 1], *lengths[dim + 2 :])


def gather_directly(value, axis, dim):
    blocks = from_everyone(value, axis)
    return in_order(blocks, dim)


def over_axes(value, axes):
    for axis in axes:
        value = lax.psum(value, axis)
    return value


def lat_halo(field):
    return with_halo(field, ((GY, 1),), 1, False)


def lon_halo(field):
    return with_halo(field, ((GX, 2),), 1, True)


def mirror(row):
    whole = gather_directly(row, GX, 1)
    width = row.shape[1]
    partner = lax.axis_size(GX) - 1 - lax.axis_index(GX)
    return lax.dynamic_slice_in_dim(whole, partner * width, width, 1)


def top_flag():
    return lax.axis_index(GY) == lax.axis_size(GY) - 1


def extend(field, signs):
    rows = lat_halo(field)
    partner_row = mirror(field[:, -1, :])
    north = signs[:, None] * partner_row[:, ::-1]
    north = jnp.where(top_flag(), north, rows[:, -1, :])
    rows = rows.at[:, -1, :].set(north)
    return lon_halo(rows)


def retract(padded_bar, signs):
    inner = padded_bar[:, :, 1:-1]
    side_rims = jnp.stack([padded_bar[:, :, 0], padded_bar[:, :, -1]], axis=2)
    side_got = lon_halo(side_rims)
    inner = inner.at[:, :, 0].add(side_got[:, :, 0])
    inner = inner.at[:, :, -1].add(side_got[:, :, 3])
    middle = inner[:, 1:-1, :]
    north_rim = inner[:, -1, :]
    row_rims = jnp.stack([inner[:, 0, :], north_rim], axis=1)
    row_got = lat_halo(row_rims)
    middle = middle.at[:, 0, :].add(row_got[:, 0, :])
    middle = middle.at[:, -1, :].add(row_got[:, 3, :])
    is_top = top_flag()
    folded = jnp.where(is_top, signs[:, None] * north_rim[:, ::-1], 0.0)
    returned = mirror(folded)
    middle = middle.at[:, -1, :].add(jnp.where(is_top, returned, 0.0))
    return middle


def centred_x(field):
    return 0.5 * (field[1:-1, 2:] - field[1:-1, :-2])


def centred_y(field):
    return 0.5 * (field[2:, 1:-1] - field[:-2, 1:-1])


def stress_update(vel_pad, stress, strength, coef):
    east = vel_pad[0]
    north = vel_pad[1]
    dudx = centred_x(east)
    dudy = centred_y(east)
    dvdx = centred_x(north)
    dvdy = centred_y(north)
    diverge = dudx + dvdy
    tension = dudx - dvdy
    shearing = dudy + dvdx
    delta = jnp.sqrt(
        diverge * diverge + (tension * tension + shearing * shearing) / ellipse_sq + delta_floor
    )
    ratio = coef * strength / delta
    denom = 1.0 + coef
    first = (stress[0] + ratio * diverge - coef * strength) / denom
    second = (stress[1] + ratio * tension / ellipse_sq) / denom
    third = (stress[2] + ratio * shearing / ellipse_sq) / denom
    return jnp.stack([first, second, third], axis=0)


def velocity_update(stress_pad, velocity, wind, mass, land):
    first = stress_pad[0]
    second = stress_pad[1]
    third = stress_pad[2]
    force_x = 0.5 * centred_x(first + second) + centred_y(third)
    force_y = 0.5 * centred_y(first - second) + centred_x(third)
    scaled = land / (mass + time_step * drag_rate)
    east = scaled * (mass * velocity[0] + time_step * (force_x + wind[0]))
    north = scaled * (mass * velocity[1] + time_step * (force_y + wind[1]))
    return jnp.stack([east, north], axis=0)


def coefficient(start_index, step):
    return 0.2 + 0.8 * (start_index[0].astype(jnp.float32) + (step + 1)) / SUBTOTAL


def per_device(
    velocity, stress, wind, strength, mass, land_mask, region_mask, observed, start_index
):
    land = land_mask.astype(jnp.float32)
    region = region_mask.astype(jnp.float32)
    vel_signs = jnp.array([-1.0, -1.0], dtype=jnp.float32)
    stress_signs = jnp.array([1.0, 1.0, 1.0], dtype=jnp.float32)
    saved = []
    vel = velocity
    sts = stress
    for step in range(STEPS):
        coef = coefficient(start_index, step)
        vel_pad = extend(vel, vel_signs)
        new_sts = stress_update(vel_pad, sts, strength, coef)
        sts_pad = extend(new_sts, stress_signs)
        new_vel = velocity_update(sts_pad, vel, wind, mass, land)
        saved.append((vel, sts))
        vel = new_vel
        sts = new_sts
    vel_bar = region * (vel - observed)
    sts_bar = jnp.zeros_like(stress)
    wind_bar = jnp.zeros_like(wind)
    for step in reversed(range(STEPS)):
        coef = coefficient(start_index, step)
        old_vel, old_sts = saved[step]
        vel_pad = extend(old_vel, vel_signs)
        sts_pad = extend(stress_update(vel_pad, old_sts, strength, coef), stress_signs)

        def move_ice(stress_ext, speed, forcing):
            return velocity_update(stress_ext, speed, forcing, mass, land)

        def relax_stress(speed_ext, previous):
            return stress_update(speed_ext, previous, strength, coef)

        unused_vel, pull_velocity = jax.vjp(move_ice, sts_pad, old_vel, wind)
        stress_ext_bar, direct_bar, wind_part = pull_velocity(vel_bar)
        wind_bar = wind_bar + wind_part
        sts_bar = sts_bar + retract(stress_ext_bar, stress_signs)
        unused_sts, pull_stress = jax.vjp(relax_stress, vel_pad, old_sts)
        speed_ext_bar, sts_bar = pull_stress(sts_bar)
        vel_bar = direct_bar + retract(speed_ext_bar, vel_signs)
    total = over_axes(jnp.sum(wind_bar * wind_bar), GX_GY)
    entries = 2 * wind_bar.shape[1] * wind_bar.shape[2] * lax.axis_size(GX) * lax.axis_size(GY)
    spread = jnp.sqrt(total / entries + norm_eps)
    state_adjoint = jnp.concatenate([vel_bar, sts_bar], axis=0)
    return (state_adjoint, wind_bar / spread)


def solution(mesh):
    finer = Mesh(mesh.devices.reshape(4, 2, 2, 4, 2), ("gx_0", "gx_1", "gx_2", "gy_0", "gy_1"))
    placed = (
        P(None, GY, GX),
        P(None, GY, GX),
        P(None, GY, GX),
        P(GY, GX),
        P(GY, GX),
        P(GY, GX),
        P(GY, GX),
        P(None, GY, GX),
        P(),
    )
    return jax.shard_map(
        per_device,
        mesh=finer,
        in_specs=placed,
        out_specs=(P(None, GY, GX), P(None, GY, GX)),
        check_vma=False,
    )
```

profile of v0, /device:TPU:0, one launch (start us, length us, event | category | flops | bytes accessed | tf_op | source)
XLA Modules:
  0.0 1015.7 jit_solution(2362307732329457696)
XLA Ops:
  5.5 6.7 all-to-all-start
  35.5 6.6 all-to-all-start.1
  42.2 7.5 all-to-all-done.1
  66.7 6.2 all-to-all-start.2
  73.0 7.5 all-to-all-done.2
  95.7 6.7 all-to-all-start.3
  102.5 7.5 all-to-all-done.3
  126.0 6.2 all-to-all-start.4
  132.3 7.5 all-to-all-done.4
  154.9 6.7 all-to-all-start.5
  161.7 7.5 all-to-all-done.5
  185.3 6.2 all-to-all-start.6
  191.6 7.5 all-to-all-done.6
  214.3 6.7 all-to-all-start.7
  221.0 7.5 all-to-all-done.7
  244.9 6.2 all-to-all-start.8
  251.2 7.5 all-to-all-done.8
  273.8 6.7 all-to-all-start.9
  280.6 7.5 all-to-all-done.9
  304.2 6.2 all-to-all-start.10
  310.5 7.5 all-to-all-done.10
  333.1 6.7 all-to-all-start.11
  339.9 7.5 all-to-all-done.11
  363.5 6.2 all-to-all-start.12
  369.8 7.5 all-to-all-done.12
  392.4 6.7 all-to-all-start.13
  399.2 7.5 all-to-all-done.13
  422.8 6.2 all-to-all-start.14
  429.2 7.5 all-to-all-done.14
  446.5 13.3 %collective-permute-start.60 = (f32[3,1,128]{2,1,0:T(1,128)S(1)}, f32[3,1,128]{2,1,0:T(1,128)S(1)}, u32[]{:S(2)}, u32[]{:S(2)}) collective-permute-start(f32[3,1,128]{2,1,0:T(1,128)S(1)} %get-tuple-element.1590), channel_id=1, source_target_pairs={{0,1},{1,2},{2,3},{3,4},{4,5},{5,6},{6,7},{8,9},{9,10},{10,11},{11... | collective-permute-start | bytes 4616 | tf_op jit(solution)/shard_map/ppermute | solution.py:28
  460.5 6.7 all-to-all-start.15
  467.3 7.5 all-to-all-done.15
  514.6 7.5 collective-permute-done.68
  527.7 7.1 all-to-all-start.17
  536.2 6.2 all-to-all-done.17
  556.8 6.9 all-to-all-start.18
  572.0 7.5 collective-permute-done.76
  584.8 7.1 all-to-all-start.19
  593.3 6.2 all-to-all-done.19
  614.2 6.9 all-to-all-start.20
  629.4 7.4 collective-permute-done.84
  639.3 7.7 scatter-add.310
  650.6 7.1 all-to-all-start.21
  657.9 7.5 all-to-all-done.21
  695.1 7.4 collective-permute-done.92
  706.1 7.7 scatter-add.326
  718.3 6.5 all-to-all-start.23
  724.9 7.5 all-to-all-done.23
  762.1 7.4 collective-permute-done.100
  772.6 7.7 scatter-add.344
  784.9 6.5 all-to-all-start.25
  791.5 7.5 all-to-all-done.25
  828.5 7.5 collective-permute-done.108
  839.5 6.8 all-to-all-start.27
  863.6 7.7 scatter-add.369
  877.0 7.0 all-to-all-start.28
  884.1 7.5 all-to-all-done.28
  892.5 7.5 collective-permute-done.116
  903.5 6.8 all-to-all-start.29
  920.2 11.5 %psum.35 = f32[]{:T(128)} all-reduce(f32[]{:T(128)} %get-tuple-element.1238), channel_id=1, replica_groups=mesh['gx_0'=4,'gx_1'=2,'gx_2'=2,'gy_0'=4,'gy_1'=2] {'gx_0'}, use_global_device_ids=true, to_apply=%region_1.2 | all-reduce | flops 1 | bytes 8 | tf_op jit(solution)/shard_map/psum | solution.py:54
  931.7 7.1 psum.36
  941.8 9.3 psum.38
  986.8 7.4 collective-permute-done.124
  999.9 7.1 all-to-all-start.31
  (876 shorter events, 541.9 us)
Async XLA Ops:
  1.4 16.3 %collective-permute-start = (f32[2,1,128]{2,1,0:T(1,128)S(1)}, f32[2,1,128]{2,1,0:T(1,128)S(1)}, u32[]{:S(2)}, u32[]{:S(2)}) collective-permute-start(f32[2,1,128]{2,1,0:T(1,128)S(1)} %get-tuple-element.1675), channel_id=1, source_target_pairs={{0,1},{1,2},{2,3},{3,4},{4,5},{5,6},{6,7},{8,9},{9,10},{10,11},{11... | collective-permute-start | bytes 3080 | tf_op jit(solution)/shard_map/ppermute | solution.py:28
  5.5 14.3 %all-to-all-start = ((f32[16,2,128]{2,1,0:T(2,128)}), f32[16,2,128]{2,1,0:T(2,128)S(1)}, u32[]{:S(2)}, u32[]{:S(2)}) async-start(f32[16,2,128]{2,1,0:T(2,128)} %broadcast_in_dim.423), calls=%async_computation | async-start | bytes 32768 | tf_op jit(solution)/shard_map/all_to_all | solution.py:38
  29.0 13.1 %collective-permute-start.5 = (f32[3,1,128]{2,0,1:T(4,128)S(1)}, f32[3,1,128]{2,0,1:T(4,128)S(1)}, u32[]{:S(2)}, u32[]{:S(2)}) collective-permute-start(f32[3,1,128]{2,0,1:T(4,128)S(1)} %copy.1801), channel_id=1, source_target_pairs={{1,0},{2,1},{3,2},{4,3},{5,4},{6,5},{7,6},{9,8},{10,9},{11,10},{12... | collective-permute-start | bytes 4616 | tf_op jit(solution)/shard_map/ppermute | solution.py:31
  30.3 11.8 %collective-permute-start.4 = (f32[3,1,128]{2,1,0:T(1,128)S(1)}, f32[3,1,128]{2,1,0:T(1,128)S(1)}, u32[]{:S(2)}, u32[]{:S(2)}) collective-permute-start(f32[3,1,128]{2,1,0:T(1,128)S(1)} %get-tuple-element.1604), channel_id=1, source_target_pairs={{0,1},{1,2},{2,3},{3,4},{4,5},{5,6},{6,7},{8,9},{9,10},{10,11},{11... | collective-permute-start | bytes 4616 | tf_op jit(solution)/shard_map/ppermute | solution.py:28
  35.5 14.2 %all-to-all-start.1 = ((f32[16,3,128]{2,1,0:T(4,128)}), f32[16,3,128]{2,1,0:T(4,128)S(1)}, u32[]{:S(2)}, u32[]{:S(2)}) async-start(f32[16,3,128]{2,1,0:T(4,128)} %broadcast_in_dim.424), calls=%async_computation.1 | async-start | bytes 65536 | tf_op jit(solution)/shard_map/all_to_all | solution.py:38
  60.3 12.7 %collective-permute-start.9 = (f32[2,1,128]{2,0,1:T(2,128)S(1)}, f32[2,1,128]{2,0,1:T(2,128)S(1)}, u32[]{:S(2)}, u32[]{:S(2)}) collective-permute-start(f32[2,1,128]{2,0,1:T(2,128)S(1)} %bitcast.1112), channel_id=1, source_target_pairs={{1,0},{2,1},{3,2},{4,3},{5,4},{6,5},{7,6},{9,8},{10,9},{11,10},{12... | collective-permute-start | bytes 3080 | tf_op jit(solution)/shard_map/ppermute | solution.py:31
  66.7 13.8 %all-to-all-start.2 = ((f32[16,2,128]{2,1,0:T(2,128)}), f32[16,2,128]{2,1,0:T(2,128)S(1)}, u32[]{:S(2)}, u32[]{:S(2)}) async-start(f32[16,2,128]{2,1,0:T(2,128)} %broadcast_in_dim.425), calls=%async_computation.2 | async-start | bytes 32768 | tf_op jit(solution)/shard_map/all_to_all | solution.py:38
  89.2 13.2 %collective-permute-start.13 = (f32[3,1,128]{2,0,1:T(4,128)S(1)}, f32[3,1,128]{2,0,1:T(4,128)S(1)}, u32[]{:S(2)}, u32[]{:S(2)}) collective-permute-start(f32[3,1,128]{2,0,1:T(4,128)S(1)} %copy.1803), channel_id=1, source_target_pairs={{1,0},{2,1},{3,2},{4,3},{5,4},{6,5},{7,6},{9,8},{10,9},{11,10},{12... | collective-permute-start | bytes 4616 | tf_op jit(solution)/shard_map/ppermute | solution.py:31
  90.5 12.0 %collective-permute-start.12 = (f32[3,1,128]{2,1,0:T(1,128)S(1)}, f32[3,1,128]{2,1,0:T(1,128)S(1)}, u32[]{:S(2)}, u32[]{:S(2)}) collective-permute-start(f32[3,1,128]{2,1,0:T(1,128)S(1)} %get-tuple-element.1602), channel_id=1, source_target_pairs={{0,1},{1,2},{2,3},{3,4},{4,5},{5,6},{6,7},{8,9},{9,10},{10,11},{11... | collective-permute-start | bytes 4616 | tf_op jit(solution)/shard_map/ppermute | solution.py:28
  95.7 14.3 %all-to-all-start.3 = ((f32[16,3,128]{2,1,0:T(4,128)}), f32[16,3,128]{2,1,0:T(4,128)S(1)}, u32[]{:S(2)}, u32[]{:S(2)}) async-start(f32[16,3,128]{2,1,0:T(4,128)} %broadcast_in_dim.426), calls=%async_computation.3 | async-start | bytes 65536 | tf_op jit(solution)/shard_map/all_to_all | solution.py:38
  119.6 12.7 %collective-permute-start.17 = (f32[2,1,128]{2,0,1:T(2,128)S(1)}, f32[2,1,128]{2,0,1:T(2,128)S(1)}, u32[]{:S(2)}, u32[]{:S(2)}) collective-permute-start(f32[2,1,128]{2,0,1:T(2,128)S(1)} %bitcast.1113), channel_id=1, source_target_pairs={{1,0},{2,1},{3,2},{4,3},{5,4},{6,5},{7,6},{9,8},{10,9},{11,10},{12... | collective-permute-start | bytes 3080 | tf_op jit(solution)/shard_map/ppermute | solution.py:31
  120.9 11.4 %collective-permute-start.16 = (f32[2,1,128]{2,1,0:T(1,128)S(1)}, f32[2,1,128]{2,1,0:T(1,128)S(1)}, u32[]{:S(2)}, u32[]{:S(2)}) collective-permute-start(f32[2,1,128]{2,1,0:T(1,128)S(1)} %get-tuple-element.1671), channel_id=1, source_target_pairs={{0,1},{1,2},{2,3},{3,4},{4,5},{5,6},{6,7},{8,9},{9,10},{10,11},{11... | collective-permute-start | bytes 3080 | tf_op jit(solution)/shard_map/ppermute | solution.py:28
  126.0 13.8 %all-to-all-start.4 = ((f32[16,2,128]{2,1,0:T(2,128)}), f32[16,2,128]{2,1,0:T(2,128)S(1)}, u32[]{:S(2)}, u32[]{:S(2)}) async-start(f32[16,2,128]{2,1,0:T(2,128)} %broadcast_in_dim.427), calls=%async_computation.4 | async-start | bytes 32768 | tf_op jit(solution)/shard_map/all_to_all | solution.py:38
  148.4 13.2 %collective-permute-start.21 = (f32[3,1,128]{2,0,1:T(4,128)S(1)}, f32[3,1,128]{2,0,1:T(4,128)S(1)}, u32[]{:S(2)}, u32[]{:S(2)}) collective-permute-start(f32[3,1,128]{2,0,1:T(4,128)S(1)} %copy.1805), channel_id=1, source_target_pairs={{1,0},{2,1},{3,2},{4,3},{5,4},{6,5},{7,6},{9,8},{10,9},{11,10},{12... | collective-permute-start | bytes 4616 | tf_op jit(solution)/shard_map/ppermute | solution.py:31
  149.7 12.0 %collective-permute-start.20 = (f32[3,1,128]{2,1,0:T(1,128)S(1)}, f32[3,1,128]{2,1,0:T(1,128)S(1)}, u32[]{:S(2)}, u32[]{:S(2)}) collective-permute-start(f32[3,1,128]{2,1,0:T(1,128)S(1)} %get-tuple-element.1600), channel_id=1, source_target_pairs={{0,1},{1,2},{2,3},{3,4},{4,5},{5,6},{6,7},{8,9},{9,10},{10,11},{11... | collective-permute-start | bytes 4616 | tf_op jit(solution)/shard_map/ppermute | solution.py:28
  154.9 14.3 %all-to-all-start.5 = ((f32[16,3,128]{2,1,0:T(4,128)}), f32[16,3,128]{2,1,0:T(4,128)S(1)}, u32[]{:S(2)}, u32[]{:S(2)}) async-start(f32[16,3,128]{2,1,0:T(4,128)} %broadcast_in_dim.428), calls=%async_computation.5 | async-start | bytes 65536 | tf_op jit(solution)/shard_map/all_to_all | solution.py:38
  178.9 12.7 %collective-permute-start.25 = (f32[2,1,128]{2,0,1:T(2,128)S(1)}, f32[2,1,128]{2,0,1:T(2,128)S(1)}, u32[]{:S(2)}, u32[]{:S(2)}) collective-permute-start(f32[2,1,128]{2,0,1:T(2,128)S(1)} %bitcast.1114), channel_id=1, source_target_pairs={{1,0},{2,1},{3,2},{4,3},{5,4},{6,5},{7,6},{9,8},{10,9},{11,10},{12... | collective-permute-start | bytes 3080 | tf_op jit(solution)/shard_map/ppermute | solution.py:31
  185.3 13.8 %all-to-all-start.6 = ((f32[16,2,128]{2,1,0:T(2,128)}), f32[16,2,128]{2,1,0:T(2,128)S(1)}, u32[]{:S(2)}, u32[]{:S(2)}) async-start(f32[16,2,128]{2,1,0:T(2,128)} %broadcast_in_dim.429), calls=%async_computation.6 | async-start | bytes 32768 | tf_op jit(solution)/shard_map/all_to_all | solution.py:38
  207.7 13.2 %collective-permute-start.29 = (f32[3,1,128]{2,0,1:T(4,128)S(1)}, f32[3,1,128]{2,0,1:T(4,128)S(1)}, u32[]{:S(2)}, u32[]{:S(2)}) collective-permute-start(f32[3,1,128]{2,0,1:T(4,128)S(1)} %copy.1807), channel_id=1, source_target_pairs={{1,0},{2,1},{3,2},{4,3},{5,4},{6,5},{7,6},{9,8},{10,9},{11,10},{12... | collective-permute-start | bytes 4616 | tf_op jit(solution)/shard_map/ppermute | solution.py:31
  209.0 12.0 %collective-permute-start.28 = (f32[3,1,128]{2,1,0:T(1,128)S(1)}, f32[3,1,128]{2,1,0:T(1,128)S(1)}, u32[]{:S(2)}, u32[]{:S(2)}) collective-permute-start(f32[3,1,128]{2,1,0:T(1,128)S(1)} %get-tuple-element.1598), channel_id=1, source_target_pairs={{0,1},{1,2},{2,3},{3,4},{4,5},{5,6},{6,7},{8,9},{9,10},{10,11},{11... | collective-permute-start | bytes 4616 | tf_op jit(solution)/shard_map/ppermute | solution.py:28
  214.3 14.3 %all-to-all-start.7 = ((f32[16,3,128]{2,1,0:T(4,128)}), f32[16,3,128]{2,1,0:T(4,128)S(1)}, u32[]{:S(2)}, u32[]{:S(2)}) async-start(f32[16,3,128]{2,1,0:T(4,128)} %broadcast_in_dim.430), calls=%async_computation.7 | async-start | bytes 65536 | tf_op jit(solution)/shard_map/all_to_all | solution.py:38
  238.4 12.7 %collective-permute-start.33 = (f32[2,1,128]{2,0,1:T(2,128)S(1)}, f32[2,1,128]{2,0,1:T(2,128)S(1)}, u32[]{:S(2)}, u32[]{:S(2)}) collective-permute-start(f32[2,1,128]{2,0,1:T(2,128)S(1)} %bitcast.1115), channel_id=1, source_target_pairs={{1,0},{2,1},{3,2},{4,3},{5,4},{6,5},{7,6},{9,8},{10,9},{11,10},{12... | collective-permute-start | bytes 3080 | tf_op jit(solution)/shard_map/ppermute | solution.py:31
  244.9 13.8 %all-to-all-start.8 = ((f32[16,2,128]{2,1,0:T(2,128)}), f32[16,2,128]{2,1,0:T(2,128)S(1)}, u32[]{:S(2)}, u32[]{:S(2)}) async-start(f32[16,2,128]{2,1,0:T(2,128)} %broadcast_in_dim.431), calls=%async_computation.8 | async-start | bytes 32768 | tf_op jit(solution)/shard_map/all_to_all | solution.py:38
  267.3 13.2 %collective-permute-start.37 = (f32[3,1,128]{2,0,1:T(4,128)S(1)}, f32[3,1,128]{2,0,1:T(4,128)S(1)}, u32[]{:S(2)}, u32[]{:S(2)}) collective-permute-start(f32[3,1,128]{2,0,1:T(4,128)S(1)} %copy.1809), channel_id=1, source_target_pairs={{1,0},{2,1},{3,2},{4,3},{5,4},{6,5},{7,6},{9,8},{10,9},{11,10},{12... | collective-permute-start | bytes 4616 | tf_op jit(solution)/shard_map/ppermute | solution.py:31
  268.6 12.0 %collective-permute-start.36 = (f32[3,1,128]{2,1,0:T(1,128)S(1)}, f32[3,1,128]{2,1,0:T(1,128)S(1)}, u32[]{:S(2)}, u32[]{:S(2)}) collective-permute-start(f32[3,1,128]{2,1,0:T(1,128)S(1)} %get-tuple-element.1596), channel_id=1, source_target_pairs={{0,1},{1,2},{2,3},{3,4},{4,5},{5,6},{6,7},{8,9},{9,10},{10,11},{11... | collective-permute-start | bytes 4616 | tf_op jit(solution)/shard_map/ppermute | solution.py:28
  273.8 14.3 %all-to-all-start.9 = ((f32[16,3,128]{2,1,0:T(4,128)}), f32[16,3,128]{2,1,0:T(4,128)S(1)}, u32[]{:S(2)}, u32[]{:S(2)}) async-start(f32[16,3,128]{2,1,0:T(4,128)} %broadcast_in_dim.432), calls=%async_computation.9 | async-start | bytes 65536 | tf_op jit(solution)/shard_map/all_to_all | solution.py:38
  297.7 12.7 %collective-permute-start.41 = (f32[2,1,128]{2,0,1:T(2,128)S(1)}, f32[2,1,128]{2,0,1:T(2,128)S(1)}, u32[]{:S(2)}, u32[]{:S(2)}) collective-permute-start(f32[2,1,128]{2,0,1:T(2,128)S(1)} %bitcast.1116), channel_id=1, source_target_pairs={{1,0},{2,1},{3,2},{4,3},{5,4},{6,5},{7,6},{9,8},{10,9},{11,10},{12... | collective-permute-start | bytes 3080 | tf_op jit(solution)/shard_map/ppermute | solution.py:31
  304.2 13.8 %all-to-all-start.10 = ((f32[16,2,128]{2,1,0:T(2,128)}), f32[16,2,128]{2,1,0:T(2,128)S(1)}, u32[]{:S(2)}, u32[]{:S(2)}) async-start(f32[16,2,128]{2,1,0:T(2,128)} %broadcast_in_dim.433), calls=%async_computation.10 | async-start | bytes 32768 | tf_op jit(solution)/shard_map/all_to_all | solution.py:38
  326.6 13.2 %collective-permute-start.45 = (f32[3,1,128]{2,0,1:T(4,128)S(1)}, f32[3,1,128]{2,0,1:T(4,128)S(1)}, u32[]{:S(2)}, u32[]{:S(2)}) collective-permute-start(f32[3,1,128]{2,0,1:T(4,128)S(1)} %copy.1811), channel_id=1, source_target_pairs={{1,0},{2,1},{3,2},{4,3},{5,4},{6,5},{7,6},{9,8},{10,9},{11,10},{12... | collective-permute-start | bytes 4616 | tf_op jit(solution)/shard_map/ppermute | solution.py:31
  327.9 12.0 %collective-permute-start.44 = (f32[3,1,128]{2,1,0:T(1,128)S(1)}, f32[3,1,128]{2,1,0:T(1,128)S(1)}, u32[]{:S(2)}, u32[]{:S(2)}) collective-permute-start(f32[3,1,128]{2,1,0:T(1,128)S(1)} %get-tuple-element.1594), channel_id=1, source_target_pairs={{0,1},{1,2},{2,3},{3,4},{4,5},{5,6},{6,7},{8,9},{9,10},{10,11},{11... | collective-permute-start | bytes 4616 | tf_op jit(solution)/shard_map/ppermute | solution.py:28
  333.1 14.3 %all-to-all-start.11 = ((f32[16,3,128]{2,1,0:T(4,128)}), f32[16,3,128]{2,1,0:T(4,128)S(1)}, u32[]{:S(2)}, u32[]{:S(2)}) async-start(f32[16,3,128]{2,1,0:T(4,128)} %broadcast_in_dim.434), calls=%async_computation.11 | async-start | bytes 65536 | tf_op jit(solution)/shard_map/all_to_all | solution.py:38
  357.0 12.7 %collective-permute-start.49 = (f32[2,1,128]{2,0,1:T(2,128)S(1)}, f32[2,1,128]{2,0,1:T(2,128)S(1)}, u32[]{:S(2)}, u32[]{:S(2)}) collective-permute-start(f32[2,1,128]{2,0,1:T(2,128)S(1)} %bitcast.1117), channel_id=1, source_target_pairs={{1,0},{2,1},{3,2},{4,3},{5,4},{6,5},{7,6},{9,8},{10,9},{11,10},{12... | collective-permute-start | bytes 3080 | tf_op jit(solution)/shard_map/ppermute | solution.py:31
  363.5 13.8 %all-to-all-start.12 = ((f32[16,2,128]{2,1,0:T(2,128)}), f32[16,2,128]{2,1,0:T(2,128)S(1)}, u32[]{:S(2)}, u32[]{:S(2)}) async-start(f32[16,2,128]{2,1,0:T(2,128)} %broadcast_in_dim.435), calls=%async_computation.12 | async-start | bytes 32768 | tf_op jit(solution)/shard_map/all_to_all | solution.py:38
  385.9 13.2 %collective-permute-start.53 = (f32[3,1,128]{2,0,1:T(4,128)S(1)}, f32[3,1,128]{2,0,1:T(4,128)S(1)}, u32[]{:S(2)}, u32[]{:S(2)}) collective-permute-start(f32[3,1,128]{2,0,1:T(4,128)S(1)} %copy.1813), channel_id=1, source_target_pairs={{1,0},{2,1},{3,2},{4,3},{5,4},{6,5},{7,6},{9,8},{10,9},{11,10},{12... | collective-permute-start | bytes 4616 | tf_op jit(solution)/shard_map/ppermute | solution.py:31
  387.2 12.0 %collective-permute-start.52 = (f32[3,1,128]{2,1,0:T(1,128)S(1)}, f32[3,1,128]{2,1,0:T(1,128)S(1)}, u32[]{:S(2)}, u32[]{:S(2)}) collective-permute-start(f32[3,1,128]{2,1,0:T(1,128)S(1)} %get-tuple-element.1592), channel_id=1, source_target_pairs={{0,1},{1,2},{2,3},{3,4},{4,5},{5,6},{6,7},{8,9},{9,10},{10,11},{11... | collective-permute-start | bytes 4616 | tf_op jit(solution)/shard_map/ppermute | solution.py:28
  392.4 14.3 %all-to-all-start.13 = ((f32[16,3,128]{2,1,0:T(4,128)}), f32[16,3,128]{2,1,0:T(4,128)S(1)}, u32[]{:S(2)}, u32[]{:S(2)}) async-start(f32[16,3,128]{2,1,0:T(4,128)} %broadcast_in_dim.436), calls=%async_computation.13 | async-start | bytes 65536 | tf_op jit(solution)/shard_map/all_to_all | solution.py:38
  416.3 12.7 %collective-permute-start.57 = (f32[2,1,128]{2,0,1:T(2,128)S(1)}, f32[2,1,128]{2,0,1:T(2,128)S(1)}, u32[]{:S(2)}, u32[]{:S(2)}) collective-permute-start(f32[2,1,128]{2,0,1:T(2,128)S(1)} %get-tuple-element.1662), channel_id=1, source_target_pairs={{1,0},{2,1},{3,2},{4,3},{5,4},{6,5},{7,6},{9,8},{10,9},{11,10},{12... | collective-permute-start | bytes 3080 | tf_op jit(solution)/shard_map/ppermute | solution.py:31
  422.8 13.8 %all-to-all-start.14 = ((f32[16,2,128]{2,1,0:T(2,128)}), f32[16,2,128]{2,1,0:T(2,128)S(1)}, u32[]{:S(2)}, u32[]{:S(2)}) async-start(f32[16,2,128]{2,1,0:T(2,128)} %broadcast_in_dim.437), calls=%async_computation.14 | async-start | bytes 32768 | tf_op jit(solution)/shard_map/all_to_all | solution.py:38
  445.2 22.0 %collective-permute-start.61 = (f32[3,1,128]{2,0,1:T(4,128)S(1)}, f32[3,1,128]{2,0,1:T(4,128)S(1)}, u32[]{:S(2)}, u32[]{:S(2)}) collective-permute-start(f32[3,1,128]{2,0,1:T(4,128)S(1)} %copy.1814), channel_id=1, source_target_pairs={{1,0},{2,1},{3,2},{4,3},{5,4},{6,5},{7,6},{9,8},{10,9},{11,10},{12... | collective-permute-start | bytes 4616 | tf_op jit(solution)/shard_map/ppermute | solution.py:31
  446.5 20.7 %collective-permute-start.60 = (f32[3,1,128]{2,1,0:T(1,128)S(1)}, f32[3,1,128]{2,1,0:T(1,128)S(1)}, u32[]{:S(2)}, u32[]{:S(2)}) collective-permute-start(f32[3,1,128]{2,1,0:T(1,128)S(1)} %get-tuple-element.1590), channel_id=1, source_target_pairs={{0,1},{1,2},{2,3},{3,4},{4,5},{5,6},{6,7},{8,9},{9,10},{10,11},{11... | collective-permute-start | bytes 4616 | tf_op jit(solution)/shard_map/ppermute | solution.py:28
  460.5 14.3 %all-to-all-start.15 = ((f32[16,3,128]{2,1,0:T(4,128)}), f32[16,3,128]{2,1,0:T(4,128)S(1)}, u32[]{:S(2)}, u32[]{:S(2)}) async-start(f32[16,3,128]{2,1,0:T(4,128)} %broadcast_in_dim.438), calls=%async_computation.15 | async-start | bytes 65536 | tf_op jit(solution)/shard_map/all_to_all | solution.py:38
  496.1 11.5 %collective-permute-start.66 = (f32[3,1,128]{2,1,0:T(1,128)S(1)}, f32[3,1,128]{2,1,0:T(1,128)S(1)}, u32[]{:S(2)}, u32[]{:S(2)}) collective-permute-start(f32[3,1,128]{2,1,0:T(1,128)S(1)} %get-tuple-element.1559), channel_id=1, source_target_pairs={{0,1},{1,2},{2,3},{3,4},{4,5},{5,6},{6,7},{8,9},{9,10},{10,11},{11... | collective-permute-start | bytes 4616 | tf_op jit(solution)/shard_map/ppermute | solution.py:28
  500.8 13.1 %all-to-all-start.16 = ((f32[16,3,128]{2,1,0:T(4,128)}), f32[16,3,128]{2,1,0:T(4,128)S(1)}, u32[]{:S(2)}, u32[]{:S(2)}) async-start(f32[16,3,128]{2,1,0:T(4,128)} %broadcast_in_dim.445), calls=%async_computation.16 | async-start | bytes 65536 | tf_op jit(solution)/shard_map/all_to_all | solution.py:38
  527.7 14.7 %all-to-all-start.17 = ((f32[16,2,128]{2,1,0:T(2,128)}), f32[16,2,128]{2,1,0:T(2,128)S(1)}, u32[]{:S(2)}, u32[]{:S(2)}) async-start(f32[16,2,128]{2,1,0:T(2,128)} %broadcast_in_dim.449), calls=%async_computation.17 | async-start | bytes 32768 | tf_op jit(solution)/shard_map/all_to_all | solution.py:38
  552.1 12.9 %collective-permute-start.74 = (f32[3,1,128]{2,1,0:T(1,128)S(1)}, f32[3,1,128]{2,1,0:T(1,128)S(1)}, u32[]{:S(2)}, u32[]{:S(2)}) collective-permute-start(f32[3,1,128]{2,1,0:T(1,128)S(1)} %get-tuple-element.1557), channel_id=1, source_target_pairs={{0,1},{1,2},{2,3},{3,4},{4,5},{5,6},{6,7},{8,9},{9,10},{10,11},{11... | collective-permute-start | bytes 4616 | tf_op jit(solution)/shard_map/ppermute | solution.py:28
  556.8 14.5 %all-to-all-start.18 = ((f32[16,3,128]{2,1,0:T(4,128)}), f32[16,3,128]{2,1,0:T(4,128)S(1)}, u32[]{:S(2)}, u32[]{:S(2)}) async-start(f32[16,3,128]{2,1,0:T(4,128)} %broadcast_in_dim.455), calls=%async_computation.18 | async-start | bytes 65536 | tf_op jit(solution)/shard_map/all_to_all | solution.py:38
  584.8 14.7 %all-to-all-start.19 = ((f32[16,2,128]{2,1,0:T(2,128)}), f32[16,2,128]{2,1,0:T(2,128)S(1)}, u32[]{:S(2)}, u32[]{:S(2)}) async-start(f32[16,2,128]{2,1,0:T(2,128)} %broadcast_in_dim.458), calls=%async_computation.19 | async-start | bytes 32768 | tf_op jit(solution)/shard_map/all_to_all | solution.py:38
  609.5 12.9 %collective-permute-start.82 = (f32[3,1,128]{2,1,0:T(1,128)S(1)}, f32[3,1,128]{2,1,0:T(1,128)S(1)}, u32[]{:S(2)}, u32[]{:S(2)}) collective-permute-start(f32[3,1,128]{2,1,0:T(1,128)S(1)} %get-tuple-element.1555), channel_id=1, source_target_pairs={{0,1},{1,2},{2,3},{3,4},{4,5},{5,6},{6,7},{8,9},{9,10},{10,11},{11... | collective-permute-start | bytes 4616 | tf_op jit(solution)/shard_map/ppermute | solution.py:28
  614.2 14.5 %all-to-all-start.20 = ((f32[16,3,128]{2,1,0:T(4,128)}), f32[16,3,128]{2,1,0:T(4,128)S(1)}, u32[]{:S(2)}, u32[]{:S(2)}) async-start(f32[16,3,128]{2,1,0:T(4,128)} %broadcast_in_dim.464), calls=%async_computation.20 | async-start | bytes 65536 | tf_op jit(solution)/shard_map/all_to_all | solution.py:38
  650.6 14.7 %all-to-all-start.21 = ((f32[16,2,128]{2,1,0:T(2,128)}), f32[16,2,128]{2,1,0:T(2,128)S(1)}, u32[]{:S(2)}, u32[]{:S(2)}) async-start(f32[16,2,128]{2,1,0:T(2,128)} %broadcast_in_dim.467), calls=%async_computation.21 | async-start | bytes 32768 | tf_op jit(solution)/shard_map/all_to_all | solution.py:38
  676.1 11.6 %collective-permute-start.90 = (f32[3,1,128]{2,1,0:T(1,128)S(1)}, f32[3,1,128]{2,1,0:T(1,128)S(1)}, u32[]{:S(2)}, u32[]{:S(2)}) collective-permute-start(f32[3,1,128]{2,1,0:T(1,128)S(1)} %get-tuple-element.1553), channel_id=1, source_target_pairs={{0,1},{1,2},{2,3},{3,4},{4,5},{5,6},{6,7},{8,9},{9,10},{10,11},{11... | collective-permute-start | bytes 4616 | tf_op jit(solution)/shard_map/ppermute | solution.py:28
  680.5 13.5 %all-to-all-start.22 = ((f32[16,3,128]{2,1,0:T(4,128)}), f32[16,3,128]{2,1,0:T(4,128)S(1)}, u32[]{:S(2)}, u32[]{:S(2)}) async-start(f32[16,3,128]{2,1,0:T(4,128)} %broadcast_in_dim.473), calls=%async_computation.22 | async-start | bytes 65536 | tf_op jit(solution)/shard_map/all_to_all | solution.py:38
  718.3 14.1 %all-to-all-start.23 = ((f32[16,2,128]{2,1,0:T(2,128)}), f32[16,2,128]{2,1,0:T(2,128)S(1)}, u32[]{:S(2)}, u32[]{:S(2)}) async-start(f32[16,2,128]{2,1,0:T(2,128)} %broadcast_in_dim.476), calls=%async_computation.23 | async-start | bytes 32768 | tf_op jit(solution)/shard_map/all_to_all | solution.py:38
  743.1 11.6 %collective-permute-start.98 = (f32[3,1,128]{2,1,0:T(1,128)S(1)}, f32[3,1,128]{2,1,0:T(1,128)S(1)}, u32[]{:S(2)}, u32[]{:S(2)}) collective-permute-start(f32[3,1,128]{2,1,0:T(1,128)S(1)} %get-tuple-element.1551), channel_id=1, source_target_pairs={{0,1},{1,2},{2,3},{3,4},{4,5},{5,6},{6,7},{8,9},{9,10},{10,11},{11... | collective-permute-start | bytes 4616 | tf_op jit(solution)/shard_map/ppermute | solution.py:28
  747.5 13.5 %all-to-all-start.24 = ((f32[16,3,128]{2,1,0:T(4,128)}), f32[16,3,128]{2,1,0:T(4,128)S(1)}, u32[]{:S(2)}, u32[]{:S(2)}) async-start(f32[16,3,128]{2,1,0:T(4,128)} %broadcast_in_dim.482), calls=%async_computation.24 | async-start | bytes 65536 | tf_op jit(solution)/shard_map/all_to_all | solution.py:38
  784.9 14.1 %all-to-all-start.25 = ((f32[16,2,128]{2,1,0:T(2,128)}), f32[16,2,128]{2,1,0:T(2,128)S(1)}, u32[]{:S(2)}, u32[]{:S(2)}) async-start(f32[16,2,128]{2,1,0:T(2,128)} %broadcast_in_dim.485), calls=%async_computation.25 | async-start | bytes 32768 | tf_op jit(solution)/shard_map/all_to_all | solution.py:38
  809.8 11.6 %collective-permute-start.106 = (f32[3,1,128]{2,1,0:T(1,128)S(1)}, f32[3,1,128]{2,1,0:T(1,128)S(1)}, u32[]{:S(2)}, u32[]{:S(2)}) collective-permute-start(f32[3,1,128]{2,1,0:T(1,128)S(1)} %get-tuple-element.1549), channel_id=1, source_target_pairs={{0,1},{1,2},{2,3},{3,4},{4,5},{5,6},{6,7},{8,9},{9,10},{10,11},{11... | collective-permute-start | bytes 4616 | tf_op jit(solution)/shard_map/ppermute | solution.py:28
  814.2 13.5 %all-to-all-start.26 = ((f32[16,3,128]{2,1,0:T(4,128)}), f32[16,3,128]{2,1,0:T(4,128)S(1)}, u32[]{:S(2)}, u32[]{:S(2)}) async-start(f32[16,3,128]{2,1,0:T(4,128)} %broadcast_in_dim.491), calls=%async_computation.26 | async-start | bytes 65536 | tf_op jit(solution)/shard_map/all_to_all | solution.py:38
  839.5 14.4 %all-to-all-start.27 = ((f32[16,2,128]{2,1,0:T(2,128)}), f32[16,2,128]{2,1,0:T(2,128)S(1)}, u32[]{:S(2)}, u32[]{:S(2)}) async-start(f32[16,2,128]{2,1,0:T(2,128)} %broadcast_in_dim.494), calls=%async_computation.27 | async-start | bytes 32768 | tf_op jit(solution)/shard_map/all_to_all | solution.py:38
  871.3 12.7 %collective-permute-start.114 = (f32[3,1,128]{2,0,1:T(4,128)S(1)}, f32[3,1,128]{2,0,1:T(4,128)S(1)}, u32[]{:S(2)}, u32[]{:S(2)}) collective-permute-start(f32[3,1,128]{2,0,1:T(4,128)S(1)} %get-tuple-element.1521), channel_id=1, source_target_pairs={{0,1},{1,2},{2,3},{3,4},{4,5},{5,6},{6,7},{8,9},{9,10},{10,11},{11... | collective-permute-start | bytes 4616 | tf_op jit(solution)/shard_map/ppermute | solution.py:28
  877.0 14.6 %all-to-all-start.28 = ((f32[16,3,128]{2,1,0:T(4,128)}), f32[16,3,128]{2,1,0:T(4,128)S(1)}, u32[]{:S(2)}, u32[]{:S(2)}) async-start(f32[16,3,128]{2,1,0:T(4,128)} %broadcast_in_dim.500), calls=%async_computation.28 | async-start | bytes 65536 | tf_op jit(solution)/shard_map/all_to_all | solution.py:38
  903.5 14.4 %all-to-all-start.29 = ((f32[16,2,128]{2,1,0:T(2,128)}), f32[16,2,128]{2,1,0:T(2,128)S(1)}, u32[]{:S(2)}, u32[]{:S(2)}) async-start(f32[16,2,128]{2,1,0:T(2,128)} %broadcast_in_dim.503), calls=%async_computation.29 | async-start | bytes 32768 | tf_op jit(solution)/shard_map/all_to_all | solution.py:38
  972.9 13.1 %all-to-all-start.30 = ((f32[16,3,128]{2,1,0:T(4,128)}), f32[16,3,128]{2,1,0:T(4,128)S(1)}, u32[]{:S(2)}, u32[]{:S(2)}) async-start(f32[16,3,128]{2,1,0:T(4,128)} %broadcast_in_dim.509), calls=%async_computation.30 | async-start | bytes 65536 | tf_op jit(solution)/shard_map/all_to_all | solution.py:38
  999.9 14.7 %all-to-all-start.31 = ((f32[16,2,128]{2,1,0:T(2,128)}), f32[16,2,128]{2,1,0:T(2,128)S(1)}, u32[]{:S(2)}, u32[]{:S(2)}) async-start(f32[16,2,128]{2,1,0:T(2,128)} %broadcast_in_dim.512), calls=%async_computation.31 | async-start | bytes 32768 | tf_op jit(solution)/shard_map/all_to_all | solution.py:38
  (104 other events, 800.3 us)
where the time goes:
time: 1020 us
  starting transfers between devices  513 us (50%)
  waiting for transfers between devices  363 us (36%)
  local copies, waits for them, and re-layouts  76.4 us (7%)
  blocking collectives  36.7 us (4%)
  other arithmetic  19.8 us (2%)
    all_to_all x32, waiting for transfers between devices, from_everyone(): return lax.all_to_all(copies, axis, split_axis=0, concat_axis=0, tiled=True)  214 us
    all_to_all x32, starting transfers between devices, from_everyone(): return lax.all_to_all(copies, axis, split_axis=0, concat_axis=0, tiled=True)  209 us
    ppermute x64, starting transfers between devices, with_halo(): lax.ppermute(lax.slice_in_dim(block, 0, width, axis=dim), axis, backward)  169 us
    ppermute x64, starting transfers between devices, with_halo(): lax.ppermute(lax.slice_in_dim(block, block.shape[dim] - width, None, axis...  136 us
    ppermute x64, waiting for transfers between devices, with_halo(): lax.ppermute(lax.slice_in_dim(block, block.shape[dim] - width, None, axis...  132 us
    psum x5, blocking collectives, over_axes(): value = lax.psum(value, axis)  36.7 us
    scatter-add x16, local copies, waits for them, and re-layouts, retract(): inner = inner.at[:, :, -1].add(side_got[:, :, 3])  36.2 us
  transfers between devices with their start and end apart: 160, of which 73 were waited for; matrix products, arithmetic and copies ran while one was open for 3% of the time, Pallas kernels for 0%

commit v1 on v0

v1 whole, which is shorter than its diff:
```python
import functools

import jax
import jax.numpy as jnp
from jax import lax
from jax.experimental import pallas as pl
from jax.experimental.pallas import tpu as pltpu
from jax.sharding import PartitionSpec as P

STEPS = 8
SUBTOTAL = 120
HALO = 2 * STEPS
LANES = 128
PAD = 8
CHUNK = 16
NORM_EPS = 1e-06
F32 = jnp.float32
MESH = pl.DeviceIdType.MESH

ROWS = 80
NORTH = slice(80, 96)
GAP = slice(96, 112)
SOUTH = slice(112, 128)
FIRST = PAD + HALO
LAST = FIRST + LANES
TALL = LAST + HALO + PAD
SIGNS = (-1.0, -1.0, 1.0, 1.0, 1.0, -1.0, -1.0, 1.0, 1.0)

N, S, E, W, NE, NW, SE, SW = range(8)


def flip_lanes(x, index):
    return jnp.take_along_axis(x, index, axis=1)


def flip_strip(strip, lane_index, sign):
    row_index = 7 - lax.broadcasted_iota(jnp.int32, (8, LANES), 0)
    upper = jnp.take_along_axis(strip[8:16], row_index, axis=0)
    lower = jnp.take_along_axis(strip[0:8], row_index, axis=0)
    upper = flip_lanes(upper, lane_index)
    lower = flip_lanes(lower, lane_index)
    return sign * upper, sign * lower


def kernel(
    nx,
    ny,
    start_ref,
    velocity,
    stress,
    wind,
    strength,
    mass,
    land,
    region,
    observed,
    state_out,
    wind_out,
    raw,
    mass_v,
    land_v,
    region_v,
    target,
    pack_e,
    pack_w,
    got_e,
    got_w,
    rev_n,
    rev_e,
    rev_w,
    field,
    static,
    saved,
    back,
    fin,
    fin_e,
    fin_w,
    got_n_f,
    got_s_f,
    got_e_f,
    got_w_f,
    got_c_f,
    red_x,
    red_y,
    load_sem,
    send_sem,
    recv_sem,
    fsend_sem,
    frecv_sem,
    self_sem,
    xs_sem,
    xr_sem,
    ys_sem,
    yr_sem,
):
    gx = lax.axis_index("gx")
    gy = lax.axis_index("gy")
    top = gy == ny - 1
    bottom = gy == 0
    not_top = gy < ny - 1
    not_bottom = gy > 0
    east = lax.rem(gx + 1, nx)
    west = lax.rem(gx + nx - 1, nx)
    fold = nx - 1 - gx
    fold_e = lax.rem(2 * nx - 2 - gx, nx)
    fold_w = lax.rem(nx - gx, nx)

    def at(x, y):
        return {"gx": x, "gy": y}

    barrier = pltpu.get_barrier_semaphore()
    for d in range(1, nx):
        pl.semaphore_signal(
            barrier, inc=1, device_id=at(lax.rem(gx + d, nx), gy), device_id_type=MESH
        )
    for d in range(1, ny):
        pl.semaphore_signal(
            barrier, inc=1, device_id=at(gx, lax.rem(gy + d, ny)), device_id_type=MESH
        )

    @pl.when(not_top)
    def _():
        for x in (east, west):
            pl.semaphore_signal(barrier, inc=1, device_id=at(x, gy + 1), device_id_type=MESH)

    @pl.when(not_bottom)
    def _():
        for x in (east, west):
            pl.semaphore_signal(barrier, inc=1, device_id=at(x, gy - 1), device_id_type=MESH)

    loads = [
        pltpu.make_async_copy(velocity, raw.at[0:2, 0:ROWS], load_sem.at[0]),
        pltpu.make_async_copy(stress, raw.at[2:5, 0:ROWS], load_sem.at[1]),
        pltpu.make_async_copy(wind, raw.at[5:7, 0:ROWS], load_sem.at[2]),
        pltpu.make_async_copy(strength, raw.at[7, 0:ROWS], load_sem.at[3]),
        pltpu.make_async_copy(mass, mass_v, load_sem.at[4]),
        pltpu.make_async_copy(land, land_v, load_sem.at[5]),
        pltpu.make_async_copy(region, region_v, load_sem.at[6]),
        pltpu.make_async_copy(observed, target.at[1:3, 0:ROWS], load_sem.at[7]),
    ]
    for copy in loads:
        copy.start()

    zero_gap = jnp.zeros((HALO, LANES), F32)
    for f in range(9):
        raw[f, GAP] = zero_gap
    for i in range(2):
        got_e[i, GAP] = zero_gap
        got_w[i, GAP] = zero_gap
    for f in range(3):
        target[f, ROWS:LANES] = jnp.zeros((LANES - ROWS, LANES), F32)
    zero_pad = jnp.zeros((PAD, LANES), F32)
    for f in range(5):
        field[f, 0:PAD] = zero_pad
        field[f, TALL - PAD : TALL] = zero_pad
    for f in range(12):
        back[f, 0:PAD] = zero_pad
        back[f, TALL - PAD : TALL] = zero_pad

    @pl.when(bottom)
    def _():
        for f in range(9):
            raw[f, SOUTH] = zero_gap
        for i in range(2):
            got_e[i, SOUTH] = zero_gap
            got_w[i, SOUTH] = zero_gap
        for f in range(7):
            got_s_f[f] = zero_gap
        got_c_f[2] = zero_gap
        got_c_f[3] = zero_gap

    for copy in loads:
        copy.wait()

    lane = lax.broadcasted_iota(jnp.int32, (ROWS, LANES), 1)
    raw[8, 0:ROWS] = land_v[...].astype(F32) * (0.5 / (mass_v[...] + 0.5))
    target[0, 0:ROWS] = region_v[...].astype(F32)
    packed_e = jnp.zeros((ROWS, LANES), F32)
    packed_w = jnp.zeros((ROWS, LANES), F32)
    for f in range(8):
        here = (lane >= HALO * f) & (lane < HALO * (f + 1))
        value = raw[f, 0:ROWS]
        packed_e = jnp.where(here, pltpu.roll(value, (HALO * f + HALO) % LANES, 1), packed_e)
        packed_w = jnp.where(here, value if f == 0 else pltpu.roll(value, HALO * f, 1), packed_w)
    pack_e[0] = packed_e
    pack_w[0] = packed_w
    pack_e[1] = pltpu.roll(raw[8, 0:ROWS], HALO, 1)
    pack_w[1] = raw[8, 0:ROWS]

    lane8 = lax.broadcasted_iota(jnp.int32, (8, LANES), 1)
    whole_flip = LANES - 1 - lane8
    group_flip = lane8 + (HALO - 1) - 2 * lax.rem(lane8, HALO)
    group = lane8 // HALO
    group_sign = jnp.where((group < 2) | ((group >= 5) & (group < 7)), -1.0, 1.0)

    @pl.when(top)
    def _():
        for f in range(9):
            rev_n[f, 0:8], rev_n[f, 8:16] = flip_strip(raw[f, 64:80], whole_flip, SIGNS[f])
        for src, dst in ((pack_e, rev_e), (pack_w, rev_w)):
            for i, sign in ((0, group_sign), (1, 1.0)):
                dst[i, 0:8], dst[i, 8:16] = flip_strip(src[i, 64:80], group_flip, sign)

    def remote(src, dst, send, recv, slot, x, y):
        return pltpu.make_async_remote_copy(
            src_ref=src,
            dst_ref=dst,
            send_sem=send.at[slot],
            recv_sem=recv.at[slot],
            device_id=at(x, y),
            device_id_type=MESH,
        )

    def exchange(send, recv, ns, e, w, corners, folded, slots):
        to_n, to_s = ns
        corner = {
            SW: (corners[0], east, gy + 1),
            SE: (corners[1], west, gy + 1),
            NW: (corners[2], east, gy - 1),
            NE: (corners[3], west, gy - 1),
        }

        def side_copies():
            return [
                remote(e, slots[W], send, recv, W, east, gy),
                remote(w, slots[E], send, recv, E, west, gy),
            ]

        def north_copies():
            return [
                remote(to_n, slots[S], send, recv, S, gx, gy + 1),
                *[remote(corner[k][0], slots[k], send, recv, k, *corner[k][1:]) for k in (SW, SE)],
            ]

        def south_copies():
            return [
                remote(to_s, slots[N], send, recv, N, gx, gy - 1),
                *[remote(corner[k][0], slots[k], send, recv, k, *corner[k][1:]) for k in (NW, NE)],
            ]

        def fold_copy(k, src, slot, x):
            return pltpu.make_async_remote_copy(
                src_ref=src,
                dst_ref=slots[slot],
                send_sem=send.at[k],
                recv_sem=recv.at[slot],
                device_id=at(x, gy),
                device_id_type=MESH,
            )

        def local_copy(i, src, slot):
            return pltpu.make_async_copy(src, slots[slot], self_sem.at[i])

        fold_n = lambda: fold_copy(S, folded[0], N, fold)
        fold_ne = lambda: fold_copy(SW, folded[1], NE, fold_e)
        fold_nw = lambda: fold_copy(SE, folded[2], NW, fold_w)
        self_ne = lambda: local_copy(0, folded[1], NE)
        self_nw = lambda: local_copy(1, folded[2], NW)

        @pl.when(not_top)
        def _():
            for copy in north_copies():
                copy.start()

        @pl.when(top)
        def _():
            fold_n().start()

        @pl.when(top & (fold_e != gx))
        def _():
            fold_ne().start()

        @pl.when(top & (fold_e == gx))
        def _():
            self_ne().start()

        @pl.when(top & (fold_w != gx))
        def _():
            fold_nw().start()

        @pl.when(top & (fold_w == gx))
        def _():
            self_nw().start()

        @pl.when(not_bottom)
        def _():
            for copy in south_copies():
                copy.start()

        for copy in side_copies():
            copy.start()

        def finish_recv():
            for copy in side_copies():
                copy.wait_recv()

            @pl.when(not_bottom)
            def _():
                for copy in north_copies():
                    copy.wait_recv()

            @pl.when(not_top)
            def _():
                for copy in south_copies():
                    copy.wait_recv()

            @pl.when(top)
            def _():
                fold_n().wait_recv()

            @pl.when(top & (fold_e != gx))
            def _():
                fold_ne().wait_recv()

            @pl.when(top & (fold_e == gx))
            def _():
                self_ne().wait()

            @pl.when(top & (fold_w != gx))
            def _():
                fold_nw().wait_recv()

            @pl.when(top & (fold_w == gx))
            def _():
                self_nw().wait()

        def finish_send():
            for copy in side_copies():
                copy.wait_send()

            @pl.when(not_top)
            def _():
                for copy in north_copies():
                    copy.wait_send()

            @pl.when(not_bottom)
            def _():
                for copy in south_copies():
                    copy.wait_send()

            @pl.when(top)
            def _():
                fold_n().wait_send()

            @pl.when(top & (fold_e != gx))
            def _():
                fold_ne().wait_send()

            @pl.when(top & (fold_w != gx))
            def _():
                fold_nw().wait_send()

        return finish_recv, finish_send

    peers = (nx - 1) + (ny - 1)
    pl.semaphore_wait(
        barrier,
        peers + 2 * not_top.astype(jnp.int32) + 2 * not_bottom.astype(jnp.int32),
    )

    finish_recv, finish_send = exchange(
        send_sem,
        recv_sem,
        (raw.at[:, 64:80], raw.at[:, 0:16]),
        pack_e,
        pack_w,
        (pack_e.at[:, 64:80], pack_w.at[:, 64:80], pack_e.at[:, 0:16], pack_w.at[:, 0:16]),
        (rev_n, rev_e, rev_w),
        {
            N: raw.at[:, NORTH],
            S: raw.at[:, SOUTH],
            E: got_e.at[:, 0:ROWS],
            W: got_w.at[:, 0:ROWS],
            NE: got_e.at[:, NORTH],
            NW: got_w.at[:, NORTH],
            SE: got_e.at[:, SOUTH],
            SW: got_w.at[:, SOUTH],
        },
    )
    finish_recv()

    centre = slice(FIRST, LAST)
    low = slice(PAD, FIRST)
    high = slice(LAST, LAST + HALO)
    whole = [jnp.transpose(raw[f]) for f in range(9)]
    halo_e = jnp.transpose(got_e[0])
    halo_w = jnp.transpose(got_w[0])
    last_e = jnp.transpose(got_e[1])[0:HALO]
    last_w = jnp.transpose(got_w[1])[0:HALO]

    def place(rows, parts):
        u, v, s1, s2, s12, wu, wv, strong, b = parts
        field[0, rows] = u
        field[1, rows] = v
        field[2, rows] = s1 + s2
        field[3, rows] = s1 - s2
        field[4, rows] = 2.0 * s12
        static[0, rows] = jnp.where(b > 0.0, 1.0, 0.0) - b
        static[1, rows] = 0.25 * b
        static[2, rows] = b * wu
        static[3, rows] = b * wv
        static[4, rows] = strong

    def split(packed, last):
        return [packed[HALO * f : HALO * (f + 1)] for f in range(8)] + [last]

    place(centre, whole)
    place(low, split(halo_w, last_w))
    place(high, split(halo_e, last_e))

    begin = start_ref[0].astype(F32)

    def coefs(k):
        step = jnp.full((CHUNK, LANES), begin + (k + 1).astype(F32), F32)
        coef = 0.2 + 0.8 * step / SUBTOTAL
        keep = 1.0 / (1.0 + coef)
        return coef, keep

    to_n = lambda x: pltpu.roll(x, LANES - 1, 1)
    to_s = lambda x: pltpu.roll(x, 1, 1)
    chunks = range(PAD, TALL - PAD, CHUNK)

    def forward(k, carry):
        coef, keep = coefs(k)
        gain = coef * keep
        for r in chunks:
            rows = slice(r, r + CHUNK)
            up = slice(r + 1, r + 1 + CHUNK)
            down = slice(r - 1, r - 1 + CHUNK)
            u = field[0, rows]
            v = field[1, rows]
            x1 = field[0, up] - field[0, down]
            x2 = field[1, up] - field[1, down]
            y1 = to_n(u) - to_s(u)
            y2 = to_n(v) - to_s(v)
            div = x1 + y2
            ten = x1 - y2
            quarter = 0.25 * ten
            half = 0.5 * (y1 + x2)
            inv = lax.rsqrt(div * div + quarter * ten + half * half + 0.16)
            rate = gain * static[4, rows]
            un = (div + quarter) * inv
            vn = (div - quarter) * inv
            sn = half * inv
            saved[k, 0, rows] = un
            saved[k, 1, rows] = vn
            saved[k, 2, rows] = sn
            saved[k, 3, rows] = rate * inv
            field[2, rows] = keep * field[2, rows] + rate * (un - 1.0)
            field[3, rows] = keep * field[3, rows] + rate * (vn - 1.0)
            field[4, rows] = keep * field[4, rows] + rate * sn
        for r in chunks:
            rows = slice(r, r + CHUNK)
            up = slice(r + 1, r + 1 + CHUNK)
            down = slice(r - 1, r - 1 + CHUNK)
            m = field[3, rows]
            q = field[4, rows]
            fx = (field[2, up] - field[2, down]) + (to_n(q) - to_s(q))
            fy = (field[4, up] - field[4, down]) + (to_n(m) - to_s(m))
            field[0, rows] = static[0, rows] * field[0, rows] + (static[2, rows] + static[1, rows] * fx)
            field[1, rows] = static[0, rows] * field[1, rows] + (static[3, rows] + static[1, rows] * fy)
        return carry

    lax.fori_loop(0, STEPS, forward, 0)

    for f in range(12):
        if f not in (7, 8, 9):
            back[f, low] = jnp.zeros((HALO, LANES), F32)
            back[f, high] = jnp.zeros((HALO, LANES), F32)
    for f in (4, 5, 6, 10, 11):
        back[f, centre] = jnp.zeros((LANES, LANES), F32)
    where_cost = jnp.transpose(target[0])
    for i in range(2):
        miss = where_cost * (field[i, centre] - jnp.transpose(target[1 + i]))
        back[i, centre] = miss
        back[2 + i, centre] = static[1, centre] * miss

    def backward(i, carry):
        k = STEPS - 1 - i
        _, keep = coefs(k)
        for r in chunks:
            rows = slice(r, r + CHUNK)
            up = slice(r + 1, r + 1 + CHUNK)
            down = slice(r - 1, r - 1 + CHUNK)
            mu = back[2, rows]
            mv = back[3, rows]
            tp = back[4, rows] + (back[2, down] - back[2, up])
            tm = back[5, rows] + (to_s(mv) - to_n(mv))
            tq = back[6, rows] + ((to_s(mu) - to_n(mu)) + (back[3, down] - back[3, up]))
            un = saved[k, 0, rows]
            vn = saved[k, 1, rows]
            sn = saved[k, 2, rows]
            g = saved[k, 3, rows]
            along = tp * un + tm * vn + tq * sn
            total = tp + tm
            quarter = 0.25 * (tp - tm)
            back[7, rows] = g * ((total + quarter) - along * un)
            back[8, rows] = g * ((total - quarter) - along * vn)
            back[9, rows] = (0.5 * g) * (tq - along * sn)
            back[4, rows] = keep * tp
            back[5, rows] = keep * tm
            back[6, rows] = keep * tq
        for r in chunks:
            rows = slice(r, r + CHUNK)
            up = slice(r + 1, r + 1 + CHUNK)
            down = slice(r - 1, r - 1 + CHUNK)
            yb = back[8, rows]
            sb = back[9, rows]
            lu = back[0, rows]
            lv = back[1, rows]
            back[10, rows] = back[10, rows] + lu
            back[11, rows] = back[11, rows] + lv
            new_u = static[0, rows] * lu + ((back[7, down] - back[7, up]) + (to_s(sb) - to_n(sb)))
            new_v = static[0, rows] * lv + ((back[9, down] - back[9, up]) + (to_s(yb) - to_n(yb)))
            back[0, rows] = new_u
            back[1, rows] = new_v
            back[2, rows] = static[1, rows] * new_u
            back[3, rows] = static[1, rows] * new_v
        return carry

    lax.fori_loop(0, STEPS, backward, 0)
    finish_send()

    def result(rows):
        b = 4.0 * static[1, rows]
        p = back[4, rows]
        m = back[5, rows]
        return [
            back[0, rows],
            back[1, rows],
            p + m,
            p - m,
            2.0 * back[6, rows],
            b * back[10, rows],
            b * back[11, rows],
        ]

    for f, value in enumerate(result(centre)):
        fin[f] = jnp.transpose(value)
    spare = [jnp.zeros((HALO, LANES), F32)]
    fin_e[...] = jnp.transpose(jnp.concatenate(result(high) + spare, axis=0))
    fin_w[...] = jnp.transpose(jnp.concatenate(result(low) + spare, axis=0))

    @pl.when(top)
    def _():
        for f in range(7):
            rev_n[f, 0:8], rev_n[f, 8:16] = flip_strip(fin[f, NORTH], whole_flip, SIGNS[f])
        for src, dst in ((fin_e, rev_e), (fin_w, rev_w)):
            dst[0, 0:8], dst[0, 8:16] = flip_strip(src[NORTH], group_flip, group_sign)

    finish_recv, finish_send = exchange(
        fsend_sem,
        frecv_sem,
        (fin.at[:, NORTH], fin.at[:, SOUTH]),
        fin_e.at[0:ROWS],
        fin_w.at[0:ROWS],
        (fin_e.at[NORTH], fin_w.at[NORTH], fin_e.at[SOUTH], fin_w.at[SOUTH]),
        (rev_n.at[0:7], rev_e.at[0], rev_w.at[0]),
        {
            N: got_n_f,
            S: got_s_f,
            E: got_e_f,
            W: got_w_f,
            NE: got_c_f.at[0],
            NW: got_c_f.at[1],
            SE: got_c_f.at[2],
            SW: got_c_f.at[3],
        },
    )
    finish_recv()
    got_e_f[64:80] = got_e_f[64:80] + got_c_f[0]
    got_w_f[64:80] = got_w_f[64:80] + got_c_f[1]
    got_e_f[0:16] = got_e_f[0:16] + got_c_f[2]
    got_w_f[0:16] = got_w_f[0:16] + got_c_f[3]

    def finished(f):
        packed_e = got_e_f[...]
        packed_w = got_w_f[...]
        side_e = pltpu.roll(packed_e, LANES - HALO - HALO * f, 1)
        side_w = packed_w if f == 0 else pltpu.roll(packed_w, LANES - HALO * f, 1)
        value = fin[f, 0:ROWS]
        value = value + jnp.where(lane >= LANES - HALO, side_e, 0.0)
        value = value + jnp.where(lane < HALO, side_w, 0.0)
        return jnp.concatenate(
            [value[0:16] + got_s_f[f], value[16:64], value[64:80] + got_n_f[f]], axis=0
        )

    grads = [finished(5), finished(6)]
    squares = grads[0] * grads[0] + grads[1] * grads[1]
    part = jnp.sum(squares, axis=0, keepdims=True)

    def all_sum(part, buf, send, recv, count, me, where):
        buf[me] = part

        def copies():
            return [
                pltpu.make_async_remote_copy(
                    src_ref=buf.at[me],
                    dst_ref=buf.at[me],
                    send_sem=send.at[d],
                    recv_sem=recv.at[d],
                    device_id=where(lax.rem(me + d, count)),
                    device_id_type=MESH,
                )
                for d in range(1, count)
            ]

        def arrivals():
            return [
                pltpu.make_async_remote_copy(
                    src_ref=buf.at[me],
                    dst_ref=buf.at[lax.rem(me + count - d, count)],
                    send_sem=send.at[d],
                    recv_sem=recv.at[d],
                    device_id=where(lax.rem(me + d, count)),
                    device_id_type=MESH,
                )
                for d in range(1, count)
            ]

        for copy in copies():
            copy.start()
        for copy in arrivals():
            copy.wait_recv()
        for copy in copies():
            copy.wait_send()
        return jnp.sum(buf[...], axis=0)

    part = all_sum(part, red_x, xs_sem, xr_sem, nx, gx, lambda j: at(j, gy))
    part = all_sum(part, red_y, ys_sem, yr_sem, ny, gy, lambda j: at(gx, j))
    for f in range(5):
        state_out[f] = finished(f)
    finish_send()
    total = jnp.sum(jnp.broadcast_to(part, (8, LANES)), axis=1, keepdims=True)[0:1]
    entries = 2 * ROWS * LANES * nx * ny
    inv = lax.rsqrt(total / entries + NORM_EPS)
    for i in range(2):
        wind_out[i] = grads[i] * inv


def solution(mesh):
    nx, ny = mesh.shape["gx"], mesh.shape["gy"]

    def per_device(velocity, stress, wind, strength, mass, land, region, observed, start):
        vm = lambda *shape: pltpu.VMEM(shape, F32)
        dma = pltpu.SemaphoreType.DMA
        any_spec = pl.BlockSpec(memory_space=pl.ANY)
        return pl.pallas_call(
            functools.partial(kernel, nx, ny),
            out_shape=(
                jax.ShapeDtypeStruct((5, ROWS, LANES), F32),
                jax.ShapeDtypeStruct((2, ROWS, LANES), F32),
            ),
            in_specs=[pl.BlockSpec(memory_space=pltpu.SMEM)] + [any_spec] * 8,
            out_specs=(
                pl.BlockSpec(memory_space=pltpu.VMEM),
                pl.BlockSpec(memory_space=pltpu.VMEM),
            ),
            scratch_shapes=[
                vm(9, LANES, LANES),
                vm(ROWS, LANES),
                pltpu.VMEM((ROWS, LANES), jnp.int32),
                pltpu.VMEM((ROWS, LANES), jnp.int32),
                vm(3, LANES, LANES),
                vm(2, ROWS, LANES),
                vm(2, ROWS, LANES),
                vm(2, LANES, LANES),
                vm(2, LANES, LANES),
                vm(9, HALO, LANES),
                vm(2, HALO, LANES),
                vm(2, HALO, LANES),
                vm(5, TALL, LANES),
                vm(5, TALL, LANES),
                vm(STEPS, 4, TALL, LANES),
                vm(12, TALL, LANES),
                vm(7, LANES, LANES),
                vm(LANES, LANES),
                vm(LANES, LANES),
                vm(7, HALO, LANES),
                vm(7, HALO, LANES),
                vm(ROWS, LANES),
                vm(ROWS, LANES),
                vm(4, HALO, LANES),
                vm(nx, 1, LANES),
                vm(ny, 1, LANES),
                dma((8,)),
                dma((8,)),
                dma((8,)),
                dma((8,)),
                dma((8,)),
                dma((2,)),
                dma((nx,)),
                dma((nx,)),
                dma((ny,)),
                dma((ny,)),
            ],
            compiler_params=pltpu.CompilerParams(
                collective_id=0, has_side_effects=True, vmem_limit_bytes=32 * 1024 * 1024
            ),
        )(start, velocity, stress, wind, strength, mass, land, region, observed)

    tri, two = P(None, "gy", "gx"), P("gy", "gx")
    return jax.shard_map(
        per_device,
        mesh=mesh,
        in_specs=(tri, tri, tri, two, two, two, two, tri, P()),
        out_specs=(tri, tri),
        check_vma=False,
    )
```

time: 1020 us -> 46 us (0.05)
  starting transfers between devices: 513 us -> 0 us
  waiting for transfers between devices: 363 us -> 0 us
  local copies, waits for them, and re-layouts: 76.4 us -> 7.98 us
  blocking collectives: 36.7 us -> 0 us
  Pallas kernels: 0 us -> 36.3 us
  other arithmetic: 19.8 us -> 0 us
    ppermute x128 -> x0, starting transfers between devices: 305 us -> none  [the longest x64 169 us: with_halo(): lax.ppermute(lax.slice_in_dim(block, 0, width, axis=dim), axis, backward)]
    all_to_all x32 -> x0, waiting for transfers between devices: 214 us -> none  [from_everyone(): return lax.all_to_all(copies, axis, split_axis=0, concat_axis=0, tiled=True)]
    all_to_all x32 -> x0, starting transfers between devices: 209 us -> none  [from_everyone(): return lax.all_to_all(copies, axis, split_axis=0, concat_axis=0, tiled=True)]
    ppermute x128 -> x0, waiting for transfers between devices: 149 us -> none  [the longest x64 132 us: with_halo(): lax.ppermute(lax.slice_in_dim(block, block.shape[dim] - width, None, axis...]
    scatter-add x72 -> x0, local copies, waits for them, and re-layouts: 46 us -> none  [the longest x16 36.2 us: retract(): inner = inner.at[:, :, -1].add(side_got[:, :, 3])]
    psum x5 -> x0, blocking collectives: 36.7 us -> none  [over_axes(): value = lax.psum(value, axis)]
    pallas_call x0 -> x1, Pallas kernels: none -> 36.3 us  [per_device(): pl.pallas_call(functools.partial(kernel, nx, ny), out_shape=(jax.ShapeDty...]
    broadcast_in_dim x36 -> x0, local copies, waits for them, and re-layouts: 20.1 us -> none  [the longest x32 19.7 us: from_everyone(): copies = jnp.broadcast_to(value, (lax.axis_size(axis), *value.shape))]
  transfers between devices with their start and end apart: 160 -> 0, of which waited for: 73 -> 0; matrix products, arithmetic and copies ran while one was open for 3% -> 0% of each run, Pallas kernels for 0% -> 0%
where the time goes in v1:
time: 46 us; the launch traced here: 45.5 us
  Pallas kernels  36.3 us (79%)
  local copies, waits for them, and re-layouts  7.98 us (17%)
  between operations  1.3 us (3%)
    pallas_call x1, Pallas kernels, per_device(): pl.pallas_call(functools.partial(kernel, nx, ny), out_shape=(jax.ShapeDty...  36.3 us
    unnamed x18, local copies, waits for them, and re-layouts  7.98 us

profile of v1, /device:TPU:0, one launch (start us, length us, event | category | flops | bytes accessed | tf_op | source)
XLA Modules:
  0.0 45.5 jit_solution(16843932348752279814)
XLA Ops:
  1.3 0.0 copy-start
  1.3 0.9 %copy-done = f32[3,80,128]{2,1,0:T(8,128)S(1)} copy-done((f32[3,80,128]{2,1,0:T(8,128)S(1)}, f32[3,80,128]{2,1,0:T(8,128)}, u32[]{:S(2)}) %copy-start) | copy-done | bytes 122904
  2.2 0.0 copy-start.1
  2.2 0.9 %copy-done.1 = f32[2,80,128]{2,1,0:T(8,128)S(1)} copy-done((f32[2,80,128]{2,1,0:T(8,128)S(1)}, f32[2,80,128]{2,1,0:T(8,128)}, u32[]{:S(2)}) %copy-start.1) | copy-done | bytes 81944
  3.1 0.0 copy-start.2
  3.1 0.9 %copy-done.2 = f32[2,80,128]{2,1,0:T(8,128)S(1)} copy-done((f32[2,80,128]{2,1,0:T(8,128)S(1)}, f32[2,80,128]{2,1,0:T(8,128)}, u32[]{:S(2)}) %copy-start.2) | copy-done | bytes 81944
  4.0 0.0 copy-start.3
  4.0 0.9 %copy-done.3 = f32[2,80,128]{2,1,0:T(8,128)S(1)} copy-done((f32[2,80,128]{2,1,0:T(8,128)S(1)}, f32[2,80,128]{2,1,0:T(8,128)}, u32[]{:S(2)}) %copy-start.3) | copy-done | bytes 81944
  4.8 0.0 copy-start.4
  4.8 0.8 %copy-done.4 = f32[80,128]{1,0:T(8,128)S(1)} copy-done((f32[80,128]{1,0:T(8,128)S(1)}, f32[80,128]{1,0:T(8,128)}, u32[]{:S(2)}) %copy-start.4) | copy-done | bytes 40984
  5.6 0.0 copy-start.5
  5.6 0.8 %copy-done.5 = f32[80,128]{1,0:T(8,128)S(1)} copy-done((f32[80,128]{1,0:T(8,128)S(1)}, f32[80,128]{1,0:T(8,128)}, u32[]{:S(2)}) %copy-start.5) | copy-done | bytes 40984
  6.4 0.0 copy-start.6
  6.4 0.8 %copy-done.6 = s32[80,128]{1,0:T(8,128)S(1)} copy-done((s32[80,128]{1,0:T(8,128)S(1)}, s32[80,128]{1,0:T(8,128)}, u32[]{:S(2)}) %copy-start.6) | copy-done | bytes 40984
  7.2 0.0 copy-start.7
  7.2 0.8 %copy-done.7 = s32[80,128]{1,0:T(8,128)S(1)} copy-done((s32[80,128]{1,0:T(8,128)S(1)}, s32[80,128]{1,0:T(8,128)}, u32[]{:S(2)}) %copy-start.7) | copy-done | bytes 40984
  8.0 36.3 %shard_map.104 = (f32[5,80,128]{2,1,0:T(8,128)S(1)}, f32[2,80,128]{2,1,0:T(8,128)S(1)}) custom-call(s32[1]{0:T(128)S(6)} %copy.13.start_ref, f32[2,80,128]{2,1,0:T(8,128)S(1)} %copy-done.1, f32[3,80,128]{2,1,0:T(8,128)S(1)} %copy-done, f32[2,80,128]{2,1,0:T(8,128)S(1)} %copy-done.2, f32[80,128]{1,0:T(8,128)S(1)} %copy-done.4, f32[80,128]{1,0:T(8,128)S(1)} %copy-done.5, ...), custom_call_target="tpu_custom_call" | custom-call | tf_op jit(solution)/shard_map/pallas_call | solution.py:648
  44.2 0.7 %copy.14 = f32[5,80,128]{2,1,0:T(8,128)} copy(f32[5,80,128]{2,1,0:T(8,128)S(1)} %get-tuple-element.4) | data formatting | bytes 409600
  44.9 0.6 %copy.15 = f32[2,80,128]{2,1,0:T(8,128)} copy(f32[2,80,128]{2,1,0:T(8,128)S(1)} %get-tuple-element.5) | data formatting | bytes 163840
Async XLA Ops:
  1.3 0.9 %copy-start = (f32[3,80,128]{2,1,0:T(8,128)S(1)}, f32[3,80,128]{2,1,0:T(8,128)}, u32[]{:S(2)}) copy-start(f32[3,80,128]{2,1,0:T(8,128)} %stress.1) | copy-start | bytes 368644
  2.2 0.9 %copy-start.1 = (f32[2,80,128]{2,1,0:T(8,128)S(1)}, f32[2,80,128]{2,1,0:T(8,128)}, u32[]{:S(2)}) copy-start(f32[2,80,128]{2,1,0:T(8,128)} %velocity.1) | copy-start | bytes 245764
  3.1 0.9 %copy-start.2 = (f32[2,80,128]{2,1,0:T(8,128)S(1)}, f32[2,80,128]{2,1,0:T(8,128)}, u32[]{:S(2)}) copy-start(f32[2,80,128]{2,1,0:T(8,128)} %wind.1) | copy-start | bytes 245764
  4.0 0.9 %copy-start.3 = (f32[2,80,128]{2,1,0:T(8,128)S(1)}, f32[2,80,128]{2,1,0:T(8,128)}, u32[]{:S(2)}) copy-start(f32[2,80,128]{2,1,0:T(8,128)} %observed.1) | copy-start | bytes 245764
  4.8 0.8 %copy-start.4 = (f32[80,128]{1,0:T(8,128)S(1)}, f32[80,128]{1,0:T(8,128)}, u32[]{:S(2)}) copy-start(f32[80,128]{1,0:T(8,128)} %strength.1) | copy-start | bytes 122884
  5.6 0.8 %copy-start.5 = (f32[80,128]{1,0:T(8,128)S(1)}, f32[80,128]{1,0:T(8,128)}, u32[]{:S(2)}) copy-start(f32[80,128]{1,0:T(8,128)} %mass.1) | copy-start | bytes 122884
  6.4 0.8 %copy-start.6 = (s32[80,128]{1,0:T(8,128)S(1)}, s32[80,128]{1,0:T(8,128)}, u32[]{:S(2)}) copy-start(s32[80,128]{1,0:T(8,128)} %land.1) | copy-start | bytes 122884
  7.2 0.8 %copy-start.7 = (s32[80,128]{1,0:T(8,128)S(1)}, s32[80,128]{1,0:T(8,128)}, u32[]{:S(2)}) copy-start(s32[80,128]{1,0:T(8,128)} %region.1) | copy-start | bytes 122884

commit v2 on v1

--- a/solution.py
+++ b/solution.py
@@ -61,13 +61,14 @@
     land_v,
     region_v,
     target,
-    pack_e,
-    pack_w,
+    bundle_e,
+    bundle_w,
+    corner_out,
     got_e,
     got_w,
+    got_c,
     rev_n,
-    rev_e,
-    rev_w,
+    rev_c,
     field,
     static,
     saved,
@@ -80,11 +81,22 @@
     got_e_f,
     got_w_f,
     got_c_f,
+    gust,
+    gust_ns,
+    got_n_w,
+    got_s_w,
+    got_e_w,
+    got_w_w,
+    got_c_w,
+    rev_n_w,
+    rev_c_w,
     red_x,
     red_y,
     load_sem,
     send_sem,
     recv_sem,
+    wsend_sem,
+    wrecv_sem,
     fsend_sem,
     frecv_sem,
     self_sem,
@@ -108,25 +120,52 @@
     def at(x, y):
         return {"gx": x, "gy": y}
 
+    cross = lax.rem(gx // 2, 2)
+    near = (gx // 4) * 2 + lax.rem(gx, 2)
+    far = cross * ny + gy
+    nears, fars = nx // 2, 2 * ny
+
+    def near_at(j):
+        return at((j // 2) * 4 + cross * 2 + lax.rem(j, 2), gy)
+
+    def far_at(j):
+        return at(gx + 2 * (j // ny - cross), lax.rem(j, ny))
+
     barrier = pltpu.get_barrier_semaphore()
-    for d in range(1, nx):
-        pl.semaphore_signal(
-            barrier, inc=1, device_id=at(lax.rem(gx + d, nx), gy), device_id_type=MESH
-        )
-    for d in range(1, ny):
-        pl.semaphore_signal(
-            barrier, inc=1, device_id=at(gx, lax.rem(gy + d, ny)), device_id_type=MESH
-        )
-
-    @pl.when(not_top)
-    def _():
-        for x in (east, west):
-            pl.semaphore_signal(barrier, inc=1, device_id=at(x, gy + 1), device_id_type=MESH)
-
-    @pl.when(not_bottom)
-    def _():
-        for x in (east, west):
-            pl.semaphore_signal(barrier, inc=1, device_id=at(x, gy - 1), device_id_type=MESH)
+
+    def greet(where):
+        pl.semaphore_signal(barrier, inc=1, device_id=where, device_id_type=MESH)
+
+    with jax.named_scope("greet"):
+        for d in range(1, fars):
+            greet(far_at(lax.rem(far + d, fars)))
+        for d in range(1, nears):
+            greet(near_at(lax.rem(near + d, nears)))
+
+        @pl.when(not_top)
+        def _():
+            for x in (east, west, gx):
+                greet(at(x, gy + 1))
+
+        @pl.when(not_bottom)
+        def _():
+            for x in (east, west, gx):
+                greet(at(x, gy - 1))
+
+        @pl.when(top)
+        def _():
+            greet(at(fold, gy))
+
+        @pl.when(top & (fold_e != gx))
+        def _():
+            greet(at(fold_e, gy))
+
+        @pl.when(top & (fold_w != gx))
+        def _():
+            greet(at(fold_w, gy))
+
+        greet(at(east, gy))
+        greet(at(west, gy))
 
     loads = [
         pltpu.make_async_copy(velocity, raw.at[0:2, 0:ROWS], load_sem.at[0]),
@@ -144,9 +183,6 @@
     zero_gap = jnp.zeros((HALO, LANES), F32)
     for f in range(9):
         raw[f, GAP] = zero_gap
-    for i in range(2):
-        got_e[i, GAP] = zero_gap
-        got_w[i, GAP] = zero_gap
     for f in range(3):
         target[f, ROWS:LANES] = jnp.zeros((LANES - ROWS, LANES), F32)
     zero_pad = jnp.zeros((PAD, LANES), F32)
@@ -154,52 +190,67 @@
         field[f, 0:PAD] = zero_pad
         field[f, TALL - PAD : TALL] = zero_pad
     for f in range(12):
-        back[f, 0:PAD] = zero_pad
-        back[f, TALL - PAD : TALL] = zero_pad
+        back[f, 0:FIRST] = jnp.zeros((FIRST, LANES), F32)
+        back[f, LAST:TALL] = jnp.zeros((FIRST, LANES), F32)
+    for f in (4, 5, 6, 10, 11):
+        back[f, FIRST:LAST] = jnp.zeros((LANES, LANES), F32)
 
     @pl.when(bottom)
     def _():
         for f in range(9):
             raw[f, SOUTH] = zero_gap
-        for i in range(2):
-            got_e[i, SOUTH] = zero_gap
-            got_w[i, SOUTH] = zero_gap
-        for f in range(7):
+        for f in range(5):
             got_s_f[f] = zero_gap
-        got_c_f[2] = zero_gap
-        got_c_f[3] = zero_gap
+        for i in (2, 3):
+            got_c[i] = jnp.zeros((2 * HALO, LANES), F32)
+            got_c_f[i] = zero_gap
+            got_c_w[i] = jnp.zeros((2, HALO, LANES), F32)
+        got_s_w[...] = jnp.zeros((2 * HALO, LANES), F32)
 
     for copy in loads:
         copy.wait()
 
     lane = lax.broadcasted_iota(jnp.int32, (ROWS, LANES), 1)
-    raw[8, 0:ROWS] = land_v[...].astype(F32) * (0.5 / (mass_v[...] + 0.5))
-    target[0, 0:ROWS] = region_v[...].astype(F32)
-    packed_e = jnp.zeros((ROWS, LANES), F32)
-    packed_w = jnp.zeros((ROWS, LANES), F32)
-    for f in range(8):
-        here = (lane >= HALO * f) & (lane < HALO * (f + 1))
-        value = raw[f, 0:ROWS]
-        packed_e = jnp.where(here, pltpu.roll(value, (HALO * f + HALO) % LANES, 1), packed_e)
-        packed_w = jnp.where(here, value if f == 0 else pltpu.roll(value, HALO * f, 1), packed_w)
-    pack_e[0] = packed_e
-    pack_w[0] = packed_w
-    pack_e[1] = pltpu.roll(raw[8, 0:ROWS], HALO, 1)
-    pack_w[1] = raw[8, 0:ROWS]
-
+    lane16 = lax.broadcasted_iota(jnp.int32, (HALO, LANES), 1)
     lane8 = lax.broadcasted_iota(jnp.int32, (8, LANES), 1)
     whole_flip = LANES - 1 - lane8
     group_flip = lane8 + (HALO - 1) - 2 * lax.rem(lane8, HALO)
     group = lane8 // HALO
     group_sign = jnp.where((group < 2) | ((group >= 5) & (group < 7)), -1.0, 1.0)
-
-    @pl.when(top)
-    def _():
-        for f in range(9):
-            rev_n[f, 0:8], rev_n[f, 8:16] = flip_strip(raw[f, 64:80], whole_flip, SIGNS[f])
-        for src, dst in ((pack_e, rev_e), (pack_w, rev_w)):
-            for i, sign in ((0, group_sign), (1, 1.0)):
-                dst[i, 0:8], dst[i, 8:16] = flip_strip(src[i, 64:80], group_flip, sign)
+    spare_rows = jnp.zeros((LANES - ROWS, LANES), F32)
+
+    with jax.named_scope("pack"):
+        drag = land_v[...].astype(F32) * (0.5 / (mass_v[...] + 0.5))
+        raw[8, 0:ROWS] = drag
+        drag_t = jnp.transpose(jnp.concatenate([drag, spare_rows], axis=0))
+        target[0, 0:ROWS] = region_v[...].astype(F32)
+        packed_e = pltpu.roll(raw[0, 0:ROWS], HALO, 1)
+        packed_w = raw[0, 0:ROWS]
+        for f in range(1, 8):
+            here = (lane >= HALO * f) & (lane < HALO * (f + 1))
+            value = raw[f, 0:ROWS]
+            packed_e = jnp.where(here, pltpu.roll(value, (HALO * f + HALO) % LANES, 1), packed_e)
+            packed_w = jnp.where(here, pltpu.roll(value, HALO * f, 1), packed_w)
+        sides = ((bundle_e, packed_e, drag_t[LANES - HALO :]), (bundle_w, packed_w, drag_t[:HALO]))
+        for i, (bundle, packed, strip) in enumerate(sides):
+            bundle[0:ROWS] = packed
+            bundle[ROWS:] = strip
+            corner_out[i, 0:HALO] = packed[64:80]
+            corner_out[i, HALO:] = pltpu.roll(strip, 48, 1)
+            corner_out[2 + i, 0:HALO] = packed[0:16]
+            corner_out[2 + i, HALO:] = pltpu.roll(strip, 80, 1)
+
+        @pl.when(top)
+        def _():
+            for f in range(9):
+                rev_n[f, 0:8], rev_n[f, 8:16] = flip_strip(raw[f, 64:80], whole_flip, SIGNS[f])
+            for i in range(2):
+                rev_c[i, 0:8], rev_c[i, 8:16] = flip_strip(
+                    corner_out[i, 0:HALO], group_flip, group_sign
+                )
+                upper, lower = flip_strip(corner_out[i, HALO:], whole_flip, 1.0)
+                rev_c[i, 16:24] = pltpu.roll(upper, 80, 1)
+                rev_c[i, 24:32] = pltpu.roll(lower, 80, 1)
 
     def remote(src, dst, send, recv, slot, x, y):
         return pltpu.make_async_remote_copy(
@@ -211,7 +262,7 @@
             device_id_type=MESH,
         )
 
-    def exchange(send, recv, ns, e, w, corners, folded, slots):
+    def exchange(turn, send, recv, ns, e, w, corners, folded, slots):
         to_n, to_s = ns
         corner = {
             SW: (corners[0], east, gy + 1),
@@ -226,17 +277,23 @@
                 remote(w, slots[E], send, recv, E, west, gy),
             ]
 
+        def corner_copy(k):
+            return remote(corner[k][0], slots[k], send, recv, k, *corner[k][1:])
+
+        def corner_copies(kinds):
+            return [corner_copy(k) for k in kinds]
+
+        def north_copy():
+            return remote(to_n, slots[S], send, recv, S, gx, gy + 1)
+
+        def south_copy():
+            return remote(to_s, slots[N], send, recv, N, gx, gy - 1)
+
         def north_copies():
-            return [
-                remote(to_n, slots[S], send, recv, S, gx, gy + 1),
-                *[remote(corner[k][0], slots[k], send, recv, k, *corner[k][1:]) for k in (SW, SE)],
-            ]
+            return [*corner_copies((SW, SE)), north_copy()]
 
         def south_copies():
-            return [
-                remote(to_s, slots[N], send, recv, N, gx, gy - 1),
-                *[remote(corner[k][0], slots[k], send, recv, k, *corner[k][1:]) for k in (NW, NE)],
-            ]
+            return [*corner_copies((NW, NE)), south_copy()]
 
         def fold_copy(k, src, slot, x):
             return pltpu.make_async_remote_copy(
@@ -249,7 +306,7 @@
             )
 
         def local_copy(i, src, slot):
-            return pltpu.make_async_copy(src, slots[slot], self_sem.at[i])
+            return pltpu.make_async_copy(src, slots[slot], self_sem.at[2 * turn + i])
 
         fold_n = lambda: fold_copy(S, folded[0], N, fold)
         fold_ne = lambda: fold_copy(SW, folded[1], NE, fold_e)
@@ -259,12 +316,13 @@
 
         @pl.when(not_top)
         def _():
-            for copy in north_copies():
+            for copy in corner_copies((SW, SE)):
                 copy.start()
 
-        @pl.when(top)
-        def _():
-            fold_n().start()
+        @pl.when(not_bottom)
+        def _():
+            for copy in corner_copies((NW, NE)):
+                copy.start()
 
         @pl.when(top & (fold_e != gx))
         def _():
@@ -281,14 +339,21 @@
         @pl.when(top & (fold_w == gx))
         def _():
             self_nw().start()
-
-        @pl.when(not_bottom)
-        def _():
-            for copy in south_copies():
-                copy.start()
 
         for copy in side_copies():
             copy.start()
+
+        @pl.when(top)
+        def _():
+            fold_n().start()
+
+        @pl.when(not_top)
+        def _():
+            north_copy().start()
+
+        @pl.when(not_bottom)
+        def _():
+            south_copy().start()
 
         def finish_recv():
             for copy in side_copies():
@@ -352,41 +417,47 @@
 
         return finish_recv, finish_send
 
-    peers = (nx - 1) + (ny - 1)
-    pl.semaphore_wait(
-        barrier,
-        peers + 2 * not_top.astype(jnp.int32) + 2 * not_bottom.astype(jnp.int32),
-    )
+    peers = (nears - 1) + (fars - 1) + 2
+    as_int = lambda flag: flag.astype(jnp.int32)
+    peers = peers + 3 * as_int(not_top) + 3 * as_int(not_bottom) + as_int(top)
+    peers = peers + as_int(top & (fold_e != gx)) + as_int(top & (fold_w != gx))
+    with jax.named_scope("barrier"):
+        pl.semaphore_wait(barrier, peers)
 
     finish_recv, finish_send = exchange(
+        0,
         send_sem,
         recv_sem,
         (raw.at[:, 64:80], raw.at[:, 0:16]),
-        pack_e,
-        pack_w,
-        (pack_e.at[:, 64:80], pack_w.at[:, 64:80], pack_e.at[:, 0:16], pack_w.at[:, 0:16]),
-        (rev_n, rev_e, rev_w),
+        bundle_e,
+        bundle_w,
+        tuple(corner_out.at[i] for i in range(4)),
+        (rev_n, rev_c.at[0], rev_c.at[1]),
         {
             N: raw.at[:, NORTH],
             S: raw.at[:, SOUTH],
-            E: got_e.at[:, 0:ROWS],
-            W: got_w.at[:, 0:ROWS],
-            NE: got_e.at[:, NORTH],
-            NW: got_w.at[:, NORTH],
-            SE: got_e.at[:, SOUTH],
-            SW: got_w.at[:, SOUTH],
+            E: got_e,
+            W: got_w,
+            NE: got_c.at[0],
+            NW: got_c.at[1],
+            SE: got_c.at[2],
+            SW: got_c.at[3],
         },
     )
-    finish_recv()
+    with jax.named_scope("recv_first"):
+        finish_recv()
 
     centre = slice(FIRST, LAST)
     low = slice(PAD, FIRST)
     high = slice(LAST, LAST + HALO)
     whole = [jnp.transpose(raw[f]) for f in range(9)]
-    halo_e = jnp.transpose(got_e[0])
-    halo_w = jnp.transpose(got_w[0])
-    last_e = jnp.transpose(got_e[1])[0:HALO]
-    last_w = jnp.transpose(got_w[1])[0:HALO]
+
+    def side(bundle, upper, lower):
+        packed = [bundle[0:ROWS], upper[0:HALO], zero_gap, lower[0:HALO]]
+        packed = jnp.transpose(jnp.concatenate(packed, axis=0))
+        strip = jnp.where(lane16 < 96, upper[HALO:], jnp.where(lane16 >= 112, lower[HALO:], 0.0))
+        strip = jnp.where(lane16 < ROWS, bundle[ROWS:], strip)
+        return [packed[HALO * f : HALO * (f + 1)] for f in range(8)] + [strip]
 
     def place(rows, parts):
         u, v, s1, s2, s12, wu, wv, strong, b = parts
@@ -401,12 +472,9 @@
         static[3, rows] = b * wv
         static[4, rows] = strong
 
-    def split(packed, last):
-        return [packed[HALO * f : HALO * (f + 1)] for f in range(8)] + [last]
-
     place(centre, whole)
-    place(low, split(halo_w, last_w))
-    place(high, split(halo_e, last_e))
+    place(low, side(got_w, got_c.at[1], got_c.at[3]))
+    place(high, side(got_e, got_c.at[0], got_c.at[2]))
 
     begin = start_ref[0].astype(F32)
 
@@ -418,9 +486,10 @@
 
     to_n = lambda x: pltpu.roll(x, LANES - 1, 1)
     to_s = lambda x: pltpu.roll(x, 1, 1)
-    chunks = range(PAD, TALL - PAD, CHUNK)
-
-    def forward(k, carry):
+    wide = range(PAD, TALL - PAD, CHUNK)
+    narrow = range(PAD + 8, TALL - PAD - 8, CHUNK)
+
+    def forward(chunks, k, carry):
         coef, keep = coefs(k)
         gain = coef * keep
         for r in chunks:
@@ -461,21 +530,17 @@
             field[1, rows] = static[0, rows] * field[1, rows] + (static[3, rows] + static[1, rows] * fy)
         return carry
 
-    lax.fori_loop(0, STEPS, forward, 0)
-
-    for f in range(12):
-        if f not in (7, 8, 9):
-            back[f, low] = jnp.zeros((HALO, LANES), F32)
-            back[f, high] = jnp.zeros((HALO, LANES), F32)
-    for f in (4, 5, 6, 10, 11):
-        back[f, centre] = jnp.zeros((LANES, LANES), F32)
+    with jax.named_scope("forward"):
+        lax.fori_loop(0, STEPS // 2, functools.partial(forward, wide), 0)
+        lax.fori_loop(STEPS // 2, STEPS, functools.partial(forward, narrow), 0)
+
     where_cost = jnp.transpose(target[0])
     for i in range(2):
         miss = where_cost * (field[i, centre] - jnp.transpose(target[1 + i]))
         back[i, centre] = miss
         back[2 + i, centre] = static[1, centre] * miss
 
-    def backward(i, carry):
+    def backward(chunks, i, carry):
         k = STEPS - 1 - i
         _, keep = coefs(k)
         for r in chunks:
@@ -518,44 +583,79 @@
             back[3, rows] = static[1, rows] * new_v
         return carry
 
-    lax.fori_loop(0, STEPS, backward, 0)
+    with jax.named_scope("backward"):
+        lax.fori_loop(0, STEPS // 2, functools.partial(backward, narrow), 0)
+        lax.fori_loop(STEPS // 2, STEPS, functools.partial(backward, wide), 0)
+
+    lane_all = lax.broadcasted_iota(jnp.int32, (LANES, LANES), 1)
+    with jax.named_scope("wind_pack"):
+        for i in range(2):
+            gust[i] = 4.0 * static[1] * back[10 + i]
+        here = ((lane_all >= 80) & (lane_all < 96)) | (lane_all >= 112)
+        both = jnp.where(here, gust[0, centre], pltpu.roll(gust[1, centre], LANES - HALO, 1))
+        gust_ns[...] = jnp.transpose(both)[64:LANES]
+
+        @pl.when(top)
+        def _():
+            for i in range(2):
+                part = slice(HALO * i, HALO * (i + 1))
+                upper, lower = flip_strip(gust_ns[part], whole_flip, -1.0)
+                rev_n_w[16 * i : 16 * i + 8] = upper
+                rev_n_w[16 * i + 8 : 16 * i + 16] = lower
+                for j, rows in ((0, high), (1, low)):
+                    upper, lower = flip_strip(gust[i, rows], whole_flip, -1.0)
+                    rev_c_w[j, i, 0:8] = pltpu.roll(upper, 80, 1)
+                    rev_c_w[j, i, 8:16] = pltpu.roll(lower, 80, 1)
+
+    finish_wind, finish_wind_send = exchange(
+        1,
+        wsend_sem,
+        wrecv_sem,
+        (gust_ns.at[0:32], gust_ns.at[32:64]),
+        gust.at[:, high],
+        gust.at[:, low],
+        (gust.at[:, high], gust.at[:, low], gust.at[:, high], gust.at[:, low]),
+        (rev_n_w, rev_c_w.at[0], rev_c_w.at[1]),
+        {
+            N: got_n_w,
+            S: got_s_w,
+            E: got_e_w,
+            W: got_w_w,
+            NE: got_c_w.at[0],
+            NW: got_c_w.at[1],
+            SE: got_c_w.at[2],
+            SW: got_c_w.at[3],
+        },
+    )
     finish_send()
 
     def result(rows):
-        b = 4.0 * static[1, rows]
         p = back[4, rows]
         m = back[5, rows]
-        return [
-            back[0, rows],
-            back[1, rows],
-            p + m,
-            p - m,
-            2.0 * back[6, rows],
-            b * back[10, rows],
-            b * back[11, rows],
-        ]
-
-    for f, value in enumerate(result(centre)):
-        fin[f] = jnp.transpose(value)
-    spare = [jnp.zeros((HALO, LANES), F32)]
-    fin_e[...] = jnp.transpose(jnp.concatenate(result(high) + spare, axis=0))
-    fin_w[...] = jnp.transpose(jnp.concatenate(result(low) + spare, axis=0))
-
-    @pl.when(top)
-    def _():
-        for f in range(7):
-            rev_n[f, 0:8], rev_n[f, 8:16] = flip_strip(fin[f, NORTH], whole_flip, SIGNS[f])
-        for src, dst in ((fin_e, rev_e), (fin_w, rev_w)):
-            dst[0, 0:8], dst[0, 8:16] = flip_strip(src[NORTH], group_flip, group_sign)
-
-    finish_recv, finish_send = exchange(
+        return [back[0, rows], back[1, rows], p + m, p - m, 2.0 * back[6, rows]]
+
+    with jax.named_scope("state_pack"):
+        for f, value in enumerate(result(centre)):
+            fin[f] = jnp.transpose(value)
+        for rows, dst in ((high, fin_e), (low, fin_w)):
+            dst[...] = jnp.transpose(jnp.concatenate(result(rows) + [spare_rows], axis=0))
+
+        @pl.when(top)
+        def _():
+            for f in range(5):
+                rev_n[f, 0:8], rev_n[f, 8:16] = flip_strip(fin[f, NORTH], whole_flip, SIGNS[f])
+            for i, src in ((0, fin_e), (1, fin_w)):
+                rev_c[i, 0:8], rev_c[i, 8:16] = flip_strip(src[NORTH], group_flip, group_sign)
+
+    finish_state, finish_state_send = exchange(
+        2,
         fsend_sem,
         frecv_sem,
         (fin.at[:, NORTH], fin.at[:, SOUTH]),
         fin_e.at[0:ROWS],
         fin_w.at[0:ROWS],
         (fin_e.at[NORTH], fin_w.at[NORTH], fin_e.at[SOUTH], fin_w.at[SOUTH]),
-        (rev_n.at[0:7], rev_e.at[0], rev_w.at[0]),
+        (rev_n.at[0:5], rev_c.at[0, 0:HALO], rev_c.at[1, 0:HALO]),
         {
             N: got_n_f,
             S: got_s_f,
@@ -567,31 +667,34 @@
             SW: got_c_f.at[3],
         },
     )
-    finish_recv()
-    got_e_f[64:80] = got_e_f[64:80] + got_c_f[0]
-    got_w_f[64:80] = got_w_f[64:80] + got_c_f[1]
-    got_e_f[0:16] = got_e_f[0:16] + got_c_f[2]
-    got_w_f[0:16] = got_w_f[0:16] + got_c_f[3]
-
-    def finished(f):
-        packed_e = got_e_f[...]
-        packed_w = got_w_f[...]
-        side_e = pltpu.roll(packed_e, LANES - HALO - HALO * f, 1)
-        side_w = packed_w if f == 0 else pltpu.roll(packed_w, LANES - HALO * f, 1)
-        value = fin[f, 0:ROWS]
-        value = value + jnp.where(lane >= LANES - HALO, side_e, 0.0)
-        value = value + jnp.where(lane < HALO, side_w, 0.0)
+    with jax.named_scope("recv_wind"):
+        finish_wind()
+
+    def with_sides(i):
+        value = gust[i, centre]
+
+        def ends(straight, upper, lower):
+            extra = jnp.where(lane16 < ROWS, straight[i], 0.0)
+            upper = pltpu.roll(upper[i], 80, 1)
+            extra = extra + jnp.where((lane16 >= 64) & (lane16 < ROWS), upper, 0.0)
+            return extra + jnp.where(lane16 < HALO, pltpu.roll(lower[i], 48, 1), 0.0)
+
+        at_w = ends(got_w_w, got_c_w.at[1], got_c_w.at[3])
+        at_e = ends(got_e_w, got_c_w.at[0], got_c_w.at[2])
+        parts = [value[:HALO] + at_w, value[HALO:-HALO], value[-HALO:] + at_e]
+        value = jnp.transpose(jnp.concatenate(parts, axis=0))
+        rows = slice(HALO * (1 - i), HALO * (2 - i))
         return jnp.concatenate(
-            [value[0:16] + got_s_f[f], value[16:64], value[64:80] + got_n_f[f]], axis=0
+            [value[0:16] + got_s_w[rows], value[16:64], value[64:80] + got_n_w[rows]], axis=0
         )
 
-    grads = [finished(5), finished(6)]
-    squares = grads[0] * grads[0] + grads[1] * grads[1]
-    part = jnp.sum(squares, axis=0, keepdims=True)
-
-    def all_sum(part, buf, send, recv, count, me, where):
-        buf[me] = part
-
+    with jax.named_scope("wind_add"):
+        for i in range(2):
+            wind_out[i] = with_sides(i)
+        squares = wind_out[0] * wind_out[0] + wind_out[1] * wind_out[1]
+        part = jnp.sum(squares, axis=0, keepdims=True)
+
+    def all_sum(buf, send, recv, count, me, where):
         def copies():
             return [
                 pltpu.make_async_remote_copy(
@@ -618,24 +721,64 @@
                 for d in range(1, count)
             ]
 
-        for copy in copies():
-            copy.start()
-        for copy in arrivals():
-            copy.wait_recv()
-        for copy in copies():
-            copy.wait_send()
-        return jnp.sum(buf[...], axis=0)
-
-    part = all_sum(part, red_x, xs_sem, xr_sem, nx, gx, lambda j: at(j, gy))
-    part = all_sum(part, red_y, ys_sem, yr_sem, ny, gy, lambda j: at(gx, j))
-    for f in range(5):
-        state_out[f] = finished(f)
-    finish_send()
+        def begin_sum(part):
+            buf[me] = part
+            for copy in copies():
+                copy.start()
+
+        def end_sum():
+            for copy in arrivals():
+                copy.wait_recv()
+            for copy in copies():
+                copy.wait_send()
+            return jnp.sum(buf[...], axis=0)
+
+        return begin_sum, end_sum
+
+    begin_near, end_near = all_sum(red_x, xs_sem, xr_sem, nears, near, near_at)
+    begin_far, end_far = all_sum(red_y, ys_sem, yr_sem, fars, far, far_at)
+    begin_near(part)
+    with jax.named_scope("recv_state"):
+        finish_state()
+    with jax.named_scope("state_add"):
+        got_e_f[64:80] = got_e_f[64:80] + got_c_f[0]
+        got_w_f[64:80] = got_w_f[64:80] + got_c_f[1]
+        got_e_f[0:16] = got_e_f[0:16] + got_c_f[2]
+        got_w_f[0:16] = got_w_f[0:16] + got_c_f[3]
+        packed_e = got_e_f[...]
+        packed_w = got_w_f[...]
+        for f in range(5):
+            side_e = pltpu.roll(packed_e, LANES - HALO - HALO * f, 1)
+            side_w = packed_w if f == 0 else pltpu.roll(packed_w, LANES - HALO * f, 1)
+            value = fin[f, 0:ROWS]
+            value = value + jnp.where(lane >= LANES - HALO, side_e, 0.0)
+            value = value + jnp.where(lane < HALO, side_w, 0.0)
+            state_out[f] = value
+            state_out[f, 0:16] = state_out[f, 0:16] + got_s_f[f]
+            state_out[f, 64:80] = state_out[f, 64:80] + got_n_f[f]
+    with jax.named_scope("sum_near"):
+        part = end_near()
+    begin_far(part)
+    finish_wind_send()
+    finish_state_send()
+    with jax.named_scope("sum_far"):
+        part = end_far()
     total = jnp.sum(jnp.broadcast_to(part, (8, LANES)), axis=1, keepdims=True)[0:1]
     entries = 2 * ROWS * LANES * nx * ny
     inv = lax.rsqrt(total / entries + NORM_EPS)
     for i in range(2):
-        wind_out[i] = grads[i] * inv
+        wind_out[i] = wind_out[i] * inv
+
+
+def writer(state, wind, state_hbm, wind_hbm, sem):
+    copies = [
+        pltpu.make_async_copy(state, state_hbm, sem.at[0]),
+        pltpu.make_async_copy(wind, wind_hbm, sem.at[1]),
+    ]
+    for copy in copies:
+        copy.start()
+    for copy in copies:
+        copy.wait()
 
 
 def solution(mesh):
@@ -645,59 +788,82 @@
         vm = lambda *shape: pltpu.VMEM(shape, F32)
         dma = pltpu.SemaphoreType.DMA
         any_spec = pl.BlockSpec(memory_space=pl.ANY)
-        return pl.pallas_call(
+        args = (velocity, stress, wind, strength, mass, land, region, observed)
+        args = [pltpu.with_memory_space_constraint(z, pltpu.HBM) for z in args]
+        shapes = (
+            jax.ShapeDtypeStruct((5, ROWS, LANES), F32),
+            jax.ShapeDtypeStruct((2, ROWS, LANES), F32),
+        )
+        vmem_spec = pl.BlockSpec(memory_space=pltpu.VMEM)
+        state, gusts = pl.pallas_call(
             functools.partial(kernel, nx, ny),
-            out_shape=(
-                jax.ShapeDtypeStruct((5, ROWS, LANES), F32),
-                jax.ShapeDtypeStruct((2, ROWS, LANES), F32),
-            ),
+            out_shape=shapes,
             in_specs=[pl.BlockSpec(memory_space=pltpu.SMEM)] + [any_spec] * 8,
-            out_specs=(
-                pl.BlockSpec(memory_space=pltpu.VMEM),
-                pl.BlockSpec(memory_space=pltpu.VMEM),
-            ),
+            out_specs=(vmem_spec, vmem_spec),
             scratch_shapes=[
                 vm(9, LANES, LANES),
                 vm(ROWS, LANES),
                 pltpu.VMEM((ROWS, LANES), jnp.int32),
                 pltpu.VMEM((ROWS, LANES), jnp.int32),
                 vm(3, LANES, LANES),
-                vm(2, ROWS, LANES),
-                vm(2, ROWS, LANES),
-                vm(2, LANES, LANES),
-                vm(2, LANES, LANES),
+                vm(ROWS + HALO, LANES),
+                vm(ROWS + HALO, LANES),
+                vm(4, 2 * HALO, LANES),
+                vm(ROWS + HALO, LANES),
+                vm(ROWS + HALO, LANES),
+                vm(4, 2 * HALO, LANES),
                 vm(9, HALO, LANES),
-                vm(2, HALO, LANES),
-                vm(2, HALO, LANES),
+                vm(2, 2 * HALO, LANES),
                 vm(5, TALL, LANES),
                 vm(5, TALL, LANES),
                 vm(STEPS, 4, TALL, LANES),
                 vm(12, TALL, LANES),
-                vm(7, LANES, LANES),
+                vm(5, LANES, LANES),
                 vm(LANES, LANES),
                 vm(LANES, LANES),
-                vm(7, HALO, LANES),
-                vm(7, HALO, LANES),
+                vm(5, HALO, LANES),
+                vm(5, HALO, LANES),
                 vm(ROWS, LANES),
                 vm(ROWS, LANES),
                 vm(4, HALO, LANES),
-                vm(nx, 1, LANES),
-                vm(ny, 1, LANES),
+                vm(2, TALL, LANES),
+                vm(64, LANES),
+                vm(2 * HALO, LANES),
+                vm(2 * HALO, LANES),
+                vm(2, HALO, LANES),
+                vm(2, HALO, LANES),
+                vm(4, 2, HALO, LANES),
+                vm(2 * HALO, LANES),
+                vm(2, 2, HALO, LANES),
+                vm(nx // 2, 1, LANES),
+                vm(2 * ny, 1, LANES),
                 dma((8,)),
                 dma((8,)),
                 dma((8,)),
                 dma((8,)),
                 dma((8,)),
-                dma((2,)),
-                dma((nx,)),
-                dma((nx,)),
-                dma((ny,)),
-                dma((ny,)),
+                dma((8,)),
+                dma((8,)),
+                dma((6,)),
+                dma((nx // 2,)),
+                dma((nx // 2,)),
+                dma((2 * ny,)),
+                dma((2 * ny,)),
             ],
             compiler_params=pltpu.CompilerParams(
                 collective_id=0, has_side_effects=True, vmem_limit_bytes=32 * 1024 * 1024
             ),
-        )(start, velocity, stress, wind, strength, mass, land, region, observed)
+        )(start, *args)
+        return pl.pallas_call(
+            writer,
+            out_shape=shapes,
+            in_specs=[vmem_spec, vmem_spec],
+            out_specs=(any_spec, any_spec),
+            scratch_shapes=[dma((2,))],
+        )(
+            pltpu.with_memory_space_constraint(state, pltpu.VMEM),
+            pltpu.with_memory_space_constraint(gusts, pltpu.VMEM),
+        )
 
     tri, two = P(None, "gy", "gx"), P("gy", "gx")
     return jax.shard_map(

time: 46 us -> 36.4 us (0.79)
  local copies, waits for them, and re-layouts: 7.98 us -> 0 us
  Pallas kernels: 36.3 us -> 34.9 us
    unnamed x18 -> x0, local copies, waits for them, and re-layouts: 7.98 us -> none
    pallas_call x1 -> x2, Pallas kernels: 36.3 us -> 34.9 us  [the longest x1 34.2 us: per_device(): pl.pallas_call(functools.partial(kernel, nx, ny), out_shape=shapes, in_sp...]
where the time goes in v2:
time: 36.4 us; the launch traced here: 36.2 us
  Pallas kernels  34.9 us (96%)
  between operations  1.29 us (4%)
    pallas_call x1, Pallas kernels, per_device(): pl.pallas_call(functools.partial(kernel, nx, ny), out_shape=shapes, in_sp...  34.2 us

profile of v2, /device:TPU:0, one launch (start us, length us, event | category | flops | bytes accessed | tf_op | source)
XLA Modules:
  0.0 36.2 jit_solution(11780446019861674974)
XLA Ops:
  1.3 34.2 %shard_map.104 = (f32[5,80,128]{2,1,0:T(8,128)S(1)}, f32[2,80,128]{2,1,0:T(8,128)S(1)}) custom-call(s32[1]{0:T(128)S(6)} %copy.11.start_ref, f32[2,80,128]{2,1,0:T(8,128)} %velocity.1, f32[3,80,128]{2,1,0:T(8,128)} %stress.1, f32[2,80,128]{2,1,0:T(8,128)} %wind.1, f32[80,128]{1,0:T(8,128)} %strength.1, f32[80,128]{1,0:T(8,128)} %mass.1, s32[80,128]{1,0:T(8,128)} %land.1, ...), custom_call_target="tpu_custom_call" | custom-call | tf_op jit(solution)/shard_map/pallas_call | solution.py:798
  35.5 0.7 %shard_map.105 = (f32[5,80,128]{2,1,0:T(8,128)}, f32[2,80,128]{2,1,0:T(8,128)}) custom-call(f32[5,80,128]{2,1,0:T(8,128)S(1)} %get-tuple-element.4.state, f32[2,80,128]{2,1,0:T(8,128)S(1)} %get-tuple-element.5.wind), custom_call_target="tpu_custom_call" | custom-call | tf_op jit(solution)/shard_map/pallas_call | solution.py:857

commit v3 on v2

--- a/solution.py
+++ b/solution.py
@@ -111,61 +111,17 @@
     bottom = gy == 0
     not_top = gy < ny - 1
     not_bottom = gy > 0
-    east = lax.rem(gx + 1, nx)
-    west = lax.rem(gx + nx - 1, nx)
+    def wrap(index, count):
+        return jnp.where(index >= count, index - count, index)
+
+    east = wrap(gx + 1, nx)
+    west = wrap(gx + nx - 1, nx)
     fold = nx - 1 - gx
-    fold_e = lax.rem(2 * nx - 2 - gx, nx)
-    fold_w = lax.rem(nx - gx, nx)
+    fold_e = wrap(2 * nx - 2 - gx, nx)
+    fold_w = wrap(nx - gx, nx)
 
     def at(x, y):
         return {"gx": x, "gy": y}
-
-    cross = lax.rem(gx // 2, 2)
-    near = (gx // 4) * 2 + lax.rem(gx, 2)
-    far = cross * ny + gy
-    nears, fars = nx // 2, 2 * ny
-
-    def near_at(j):
-        return at((j // 2) * 4 + cross * 2 + lax.rem(j, 2), gy)
-
-    def far_at(j):
-        return at(gx + 2 * (j // ny - cross), lax.rem(j, ny))
-
-    barrier = pltpu.get_barrier_semaphore()
-
-    def greet(where):
-        pl.semaphore_signal(barrier, inc=1, device_id=where, device_id_type=MESH)
-
-    with jax.named_scope("greet"):
-        for d in range(1, fars):
-            greet(far_at(lax.rem(far + d, fars)))
-        for d in range(1, nears):
-            greet(near_at(lax.rem(near + d, nears)))
-
-        @pl.when(not_top)
-        def _():
-            for x in (east, west, gx):
-                greet(at(x, gy + 1))
-
-        @pl.when(not_bottom)
-        def _():
-            for x in (east, west, gx):
-                greet(at(x, gy - 1))
-
-        @pl.when(top)
-        def _():
-            greet(at(fold, gy))
-
-        @pl.when(top & (fold_e != gx))
-        def _():
-            greet(at(fold_e, gy))
-
-        @pl.when(top & (fold_w != gx))
-        def _():
-            greet(at(fold_w, gy))
-
-        greet(at(east, gy))
-        greet(at(west, gy))
 
     loads = [
         pltpu.make_async_copy(velocity, raw.at[0:2, 0:ROWS], load_sem.at[0]),
@@ -179,6 +135,60 @@
     ]
     for copy in loads:
         copy.start()
+
+    ring = lax.div(gx, 4)
+    core = lax.rem(gx, 2)
+    cross = lax.div(gx - 4 * ring - core, 2)
+    rings = nx // 4
+    near = ring * 2 + core
+    far = cross * ny + gy
+    nears, fars = 2 * rings, 2 * ny
+
+    def near_at(d, sign=1):
+        r = wrap(ring + (d // 2 if sign > 0 else rings - d // 2), rings) if d // 2 else ring
+        c = 1 - core if d % 2 else core
+        return r * 2 + c, at(r * 4 + cross * 2 + c, gy)
+
+    def far_at(d, sign=1):
+        y = wrap(gy + (d // 2 if sign > 0 else ny - d // 2), ny) if d // 2 else gy
+        x = 1 - cross if d % 2 else cross
+        return x * ny + y, at(gx + 2 * (x - cross), y)
+
+    barrier = pltpu.get_barrier_semaphore()
+
+    def greet(where):
+        pl.semaphore_signal(barrier, inc=1, device_id=where, device_id_type=MESH)
+
+    with jax.named_scope("greet"):
+        greet(at(east, gy))
+        greet(at(west, gy))
+
+        @pl.when(not_top)
+        def _():
+            for x in (gx, east, west):
+                greet(at(x, gy + 1))
+
+        @pl.when(not_bottom)
+        def _():
+            for x in (gx, east, west):
+                greet(at(x, gy - 1))
+
+        @pl.when(top)
+        def _():
+            greet(at(fold, gy))
+
+        @pl.when(top & (fold_e != gx))
+        def _():
+            greet(at(fold_e, gy))
+
+        @pl.when(top & (fold_w != gx))
+        def _():
+            greet(at(fold_w, gy))
+
+        for d in range(1, fars):
+            greet(far_at(d)[1])
+        for d in range(1, nears):
+            greet(near_at(d)[1])
 
     zero_gap = jnp.zeros((HALO, LANES), F32)
     for f in range(9):
@@ -479,7 +489,7 @@
     begin = start_ref[0].astype(F32)
 
     def coefs(k):
-        step = jnp.full((CHUNK, LANES), begin + (k + 1).astype(F32), F32)
+        step = jnp.full((CHUNK, LANES), begin + jnp.asarray(k + 1, jnp.int32).astype(F32), F32)
         coef = 0.2 + 0.8 * step / SUBTOTAL
         keep = 1.0 / (1.0 + coef)
         return coef, keep
@@ -531,8 +541,8 @@
         return carry
 
     with jax.named_scope("forward"):
-        lax.fori_loop(0, STEPS // 2, functools.partial(forward, wide), 0)
-        lax.fori_loop(STEPS // 2, STEPS, functools.partial(forward, narrow), 0)
+        lax.fori_loop(0, STEPS // 2, functools.partial(forward, wide), 0, unroll=4)
+        lax.fori_loop(STEPS // 2, STEPS, functools.partial(forward, narrow), 0, unroll=4)
 
     where_cost = jnp.transpose(target[0])
     for i in range(2):
@@ -540,7 +550,7 @@
         back[i, centre] = miss
         back[2 + i, centre] = static[1, centre] * miss
 
-    def backward(chunks, i, carry):
+    def backward(chunks, last, i, carry):
         k = STEPS - 1 - i
         _, keep = coefs(k)
         for r in chunks:
@@ -573,24 +583,26 @@
             sb = back[9, rows]
             lu = back[0, rows]
             lv = back[1, rows]
-            back[10, rows] = back[10, rows] + lu
-            back[11, rows] = back[11, rows] + lv
+            if not last:
+                back[10, rows] = back[10, rows] + lu
+                back[11, rows] = back[11, rows] + lv
             new_u = static[0, rows] * lu + ((back[7, down] - back[7, up]) + (to_s(sb) - to_n(sb)))
             new_v = static[0, rows] * lv + ((back[9, down] - back[9, up]) + (to_s(yb) - to_n(yb)))
             back[0, rows] = new_u
             back[1, rows] = new_v
-            back[2, rows] = static[1, rows] * new_u
-            back[3, rows] = static[1, rows] * new_v
+            if not last:
+                back[2, rows] = static[1, rows] * new_u
+                back[3, rows] = static[1, rows] * new_v
         return carry
 
     with jax.named_scope("backward"):
-        lax.fori_loop(0, STEPS // 2, functools.partial(backward, narrow), 0)
-        lax.fori_loop(STEPS // 2, STEPS, functools.partial(backward, wide), 0)
+        lax.fori_loop(0, STEPS // 2, functools.partial(backward, narrow, False), 0, unroll=4)
+        lax.fori_loop(STEPS // 2, STEPS - 1, functools.partial(backward, wide, False), 0, unroll=3)
 
     lane_all = lax.broadcasted_iota(jnp.int32, (LANES, LANES), 1)
     with jax.named_scope("wind_pack"):
         for i in range(2):
-            gust[i] = 4.0 * static[1] * back[10 + i]
+            gust[i] = 4.0 * static[1] * (back[10 + i] + back[i])
         here = ((lane_all >= 80) & (lane_all < 96)) | (lane_all >= 112)
         both = jnp.where(here, gust[0, centre], pltpu.roll(gust[1, centre], LANES - HALO, 1))
         gust_ns[...] = jnp.transpose(both)[64:LANES]
@@ -627,6 +639,8 @@
             SW: got_c_w.at[3],
         },
     )
+    with jax.named_scope("backward_last"):
+        backward(wide, True, STEPS - 1, 0)
     finish_send()
 
     def result(rows):
@@ -647,6 +661,67 @@
             for i, src in ((0, fin_e), (1, fin_w)):
                 rev_c[i, 0:8], rev_c[i, 8:16] = flip_strip(src[NORTH], group_flip, group_sign)
 
+    with jax.named_scope("recv_wind"):
+        finish_wind()
+
+    def with_sides(i):
+        value = gust[i, centre]
+
+        def ends(straight, upper, lower):
+            extra = jnp.where(lane16 < ROWS, straight[i], 0.0)
+            upper = pltpu.roll(upper[i], 80, 1)
+            extra = extra + jnp.where((lane16 >= 64) & (lane16 < ROWS), upper, 0.0)
+            return extra + jnp.where(lane16 < HALO, pltpu.roll(lower[i], 48, 1), 0.0)
+
+        at_w = ends(got_w_w, got_c_w.at[1], got_c_w.at[3])
+        at_e = ends(got_e_w, got_c_w.at[0], got_c_w.at[2])
+        parts = [value[:HALO] + at_w, value[HALO:-HALO], value[-HALO:] + at_e]
+        value = jnp.transpose(jnp.concatenate(parts, axis=0))
+        rows = slice(HALO * (1 - i), HALO * (2 - i))
+        return jnp.concatenate(
+            [value[0:16] + got_s_w[rows], value[16:64], value[64:80] + got_n_w[rows]], axis=0
+        )
+
+    with jax.named_scope("wind_add"):
+        for i in range(2):
+            wind_out[i] = with_sides(i)
+        squares = wind_out[0] * wind_out[0] + wind_out[1] * wind_out[1]
+        part = jnp.sum(squares, axis=0, keepdims=True)
+
+    def all_sum(buf, send, recv, count, me, where):
+        def copy_of(d, slot):
+            return pltpu.make_async_remote_copy(
+                src_ref=buf.at[me],
+                dst_ref=buf.at[slot],
+                send_sem=send.at[d],
+                recv_sem=recv.at[d],
+                device_id=where(d)[1],
+                device_id_type=MESH,
+            )
+
+        def copies():
+            return [copy_of(d, me) for d in range(1, count)]
+
+        def arrivals():
+            return [copy_of(d, where(d, -1)[0]) for d in range(1, count)]
+
+        def begin_sum(part):
+            buf[me] = part
+            for copy in copies():
+                copy.start()
+
+        def end_sum():
+            for copy in arrivals():
+                copy.wait_recv()
+            for copy in copies():
+                copy.wait_send()
+            return jnp.sum(buf[...], axis=0)
+
+        return begin_sum, end_sum
+
+    begin_near, end_near = all_sum(red_x, xs_sem, xr_sem, nears, near, near_at)
+    begin_far, end_far = all_sum(red_y, ys_sem, yr_sem, fars, far, far_at)
+    begin_near(part)
     finish_state, finish_state_send = exchange(
         2,
         fsend_sem,
@@ -667,77 +742,9 @@
             SW: got_c_f.at[3],
         },
     )
-    with jax.named_scope("recv_wind"):
-        finish_wind()
-
-    def with_sides(i):
-        value = gust[i, centre]
-
-        def ends(straight, upper, lower):
-            extra = jnp.where(lane16 < ROWS, straight[i], 0.0)
-            upper = pltpu.roll(upper[i], 80, 1)
-            extra = extra + jnp.where((lane16 >= 64) & (lane16 < ROWS), upper, 0.0)
-            return extra + jnp.where(lane16 < HALO, pltpu.roll(lower[i], 48, 1), 0.0)
-
-        at_w = ends(got_w_w, got_c_w.at[1], got_c_w.at[3])
-        at_e = ends(got_e_w, got_c_w.at[0], got_c_w.at[2])
-        parts = [value[:HALO] + at_w, value[HALO:-HALO], value[-HALO:] + at_e]
-        value = jnp.transpose(jnp.concatenate(parts, axis=0))
-        rows = slice(HALO * (1 - i), HALO * (2 - i))
-        return jnp.concatenate(
-            [value[0:16] + got_s_w[rows], value[16:64], value[64:80] + got_n_w[rows]], axis=0
-        )
-
-    with jax.named_scope("wind_add"):
-        for i in range(2):
-            wind_out[i] = with_sides(i)
-        squares = wind_out[0] * wind_out[0] + wind_out[1] * wind_out[1]
-        part = jnp.sum(squares, axis=0, keepdims=True)
-
-    def all_sum(buf, send, recv, count, me, where):
-        def copies():
-            return [
-                pltpu.make_async_remote_copy(
-                    src_ref=buf.at[me],
-                    dst_ref=buf.at[me],
-                    send_sem=send.at[d],
-                    recv_sem=recv.at[d],
-                    device_id=where(lax.rem(me + d, count)),
-                    device_id_type=MESH,
-                )
-                for d in range(1, count)
-            ]
-
-        def arrivals():
-            return [
-                pltpu.make_async_remote_copy(
-                    src_ref=buf.at[me],
-                    dst_ref=buf.at[lax.rem(me + count - d, count)],
-                    send_sem=send.at[d],
-                    recv_sem=recv.at[d],
-                    device_id=where(lax.rem(me + d, count)),
-                    device_id_type=MESH,
-                )
-                for d in range(1, count)
-            ]
-
-        def begin_sum(part):
-            buf[me] = part
-            for copy in copies():
-                copy.start()
-
-        def end_sum():
-            for copy in arrivals():
-                copy.wait_recv()
-            for copy in copies():
-                copy.wait_send()
-            return jnp.sum(buf[...], axis=0)
-
-        return begin_sum, end_sum
-
-    begin_near, end_near = all_sum(red_x, xs_sem, xr_sem, nears, near, near_at)
-    begin_far, end_far = all_sum(red_y, ys_sem, yr_sem, fars, far, far_at)
-    begin_near(part)
+    with jax.named_scope("sum_near"):
+        part = end_near()
+    begin_far(part)
     with jax.named_scope("recv_state"):
         finish_state()
     with jax.named_scope("state_add"):
@@ -756,9 +763,6 @@
             state_out[f] = value
             state_out[f, 0:16] = state_out[f, 0:16] + got_s_f[f]
             state_out[f, 64:80] = state_out[f, 64:80] + got_n_f[f]
-    with jax.named_scope("sum_near"):
-        part = end_near()
-    begin_far(part)
     finish_wind_send()
     finish_state_send()
     with jax.named_scope("sum_far"):
@@ -771,9 +775,10 @@
 
 
 def writer(state, wind, state_hbm, wind_hbm, sem):
+    pieces = [(state, state_hbm, f) for f in range(5)] + [(wind, wind_hbm, f) for f in range(2)]
     copies = [
-        pltpu.make_async_copy(state, state_hbm, sem.at[0]),
-        pltpu.make_async_copy(wind, wind_hbm, sem.at[1]),
+        pltpu.make_async_copy(src.at[f], dst.at[f], sem.at[i])
+        for i, (src, dst, f) in enumerate(pieces)
     ]
     for copy in copies:
         copy.start()
@@ -788,8 +793,8 @@
         vm = lambda *shape: pltpu.VMEM(shape, F32)
         dma = pltpu.SemaphoreType.DMA
         any_spec = pl.BlockSpec(memory_space=pl.ANY)
-        args = (velocity, stress, wind, strength, mass, land, region, observed)
-        args = [pltpu.with_memory_space_constraint(z, pltpu.HBM) for z in args]
+        args = (start, velocity, stress, wind, strength, mass, land, region, observed)
+        args = [args[0]] + [pltpu.with_memory_space_constraint(z, pltpu.HBM) for z in args[1:]]
         shapes = (
             jax.ShapeDtypeStruct((5, ROWS, LANES), F32),
             jax.ShapeDtypeStruct((2, ROWS, LANES), F32),
@@ -837,7 +842,7 @@
                 vm(2, 2, HALO, LANES),
                 vm(nx // 2, 1, LANES),
                 vm(2 * ny, 1, LANES),
-                dma((8,)),
+                dma((9,)),
                 dma((8,)),
                 dma((8,)),
                 dma((8,)),
@@ -853,13 +858,13 @@
             compiler_params=pltpu.CompilerParams(
                 collective_id=0, has_side_effects=True, vmem_limit_bytes=32 * 1024 * 1024
             ),
-        )(start, *args)
+        )(*args)
         return pl.pallas_call(
             writer,
             out_shape=shapes,
             in_specs=[vmem_spec, vmem_spec],
             out_specs=(any_spec, any_spec),
-            scratch_shapes=[dma((2,))],
+            scratch_shapes=[dma((7,))],
         )(
             pltpu.with_memory_space_constraint(state, pltpu.VMEM),
             pltpu.with_memory_space_constraint(gusts, pltpu.VMEM),

time: 36.4 us -> 33.6 us (0.923)
  Pallas kernels: 34.9 us -> 32.2 us
    pallas_call x1, Pallas kernels: 34.2 us -> 31.5 us  [per_device(): pl.pallas_call(functools.partial(kernel, nx, ny), out_shape=shapes, in_sp...]
where the time goes in v3:
time: 33.6 us; the launch traced here: 33.5 us
  Pallas kernels  32.2 us (96%)
  between operations  1.29 us (4%)
    pallas_call x1, Pallas kernels, per_device(): pl.pallas_call(functools.partial(kernel, nx, ny), out_shape=shapes, in_sp...  31.5 us
    pallas_call x1, Pallas kernels, per_device(): pl.pallas_call(writer, out_shape=shapes, in_specs=[vmem_spec, vmem_spec],...  0.76 us

profile of v3, /device:TPU:0, one launch (start us, length us, event | category | flops | bytes accessed | tf_op | source)
XLA Modules:
  0.0 33.5 jit_solution(11187950586325262039)
XLA Ops:
  1.3 31.5 %shard_map.104 = (f32[5,80,128]{2,1,0:T(8,128)S(1)}, f32[2,80,128]{2,1,0:T(8,128)S(1)}) custom-call(s32[1]{0:T(128)S(6)} %copy.11.start_ref, f32[2,80,128]{2,1,0:T(8,128)} %velocity.1, f32[3,80,128]{2,1,0:T(8,128)} %stress.1, f32[2,80,128]{2,1,0:T(8,128)} %wind.1, f32[80,128]{1,0:T(8,128)} %strength.1, f32[80,128]{1,0:T(8,128)} %mass.1, s32[80,128]{1,0:T(8,128)} %land.1, ...), custom_call_target="tpu_custom_call" | custom-call | tf_op jit(solution)/shard_map/pallas_call | solution.py:803
  32.7 0.8 %shard_map.105 = (f32[5,80,128]{2,1,0:T(8,128)}, f32[2,80,128]{2,1,0:T(8,128)}) custom-call(f32[5,80,128]{2,1,0:T(8,128)S(1)} %get-tuple-element.4.state, f32[2,80,128]{2,1,0:T(8,128)S(1)} %get-tuple-element.5.wind), custom_call_target="tpu_custom_call" | custom-call | tf_op jit(solution)/shard_map/pallas_call | solution.py:862
